TPU v7x, 32 devices: a whole 2x2x4 slice. The times are simulated.
32 devices in a mesh: shard: 8 (over z, y), model: 4 (over x, core).
Axes of the slice: x: 2, y: 2, z: 4, core: 2. Of those that a mesh axis runs over, the one named last changes fastest.
Arguments:
- one_gate: float32 [2048, 8192], P('shard', 'model'), may hold values from -0.1875 to 0.1875
- other_gate: float32 [2048, 8192], P('shard', 'model'), may hold values from -0.125 to 0.125
- one_up: float32 [2048, 8192], P('shard', 'model'), may hold values from -0.1875 to 0.1875
- other_up: float32 [2048, 8192], P('shard', 'model'), may hold values from -0.125 to 0.125
- mix_share: float32 [2048], P('shard'), may hold values from 0.2 to 0.8
- norm_train: float32 [2048], P(('shard', 'model')), may hold values from 0.25 to 1.75
- norm_step: float32 [2048], P(('shard', 'model')), may hold values from -0.3 to 0.3
Outputs:
- final_gate: bfloat16 [2048, 8192], P(None, 'model')
- final_up: bfloat16 [2048, 8192], P(None, 'model')
- column_gate: float32 [8192], P('model')
- column_up: float32 [8192], P('model')
- serve_norm: bfloat16 [2048], replicated
All inputs are finite; a program needn't handle non-finite values. Where the computation divides by a largest or mean magnitude, that divisor is 1e-20 or more.
Results may differ from a plain program's by a relative error of at most 0.001.
Values may be sent and summed in bfloat16 or wider, within the bound.
A program may use at most 128 MiB of HBM per device.

v0:
```python
import functools

import jax
import jax.numpy as jnp
from jax import lax
from jax.experimental import pallas as pl
from jax.experimental.pallas import tpu as pltpu
from jax.sharding import PartitionSpec as P

MESH = pl.DeviceIdType.MESH
LANES = 128


def position_of(index, n):
    return jnp.where(index % 2 == 0, index // 2, n - 1 - index // 2)


def index_at(position, n):
    return jnp.where(position < n // 2, 2 * position, 2 * (n - 1 - position) + 1)


def kernel(
    n, k, parts,
    one_gate, other_gate, one_up, other_up, mix, norm_train, norm_step,
    final_gate, final_up, column_gate, column_up, serve_norm,
    held_one, held_other, share, maxima, gains, gain_rows,
    load_sem, max_send, max_recv, norm_send, norm_recv, ring_send, ring_recv,
):
    rows, cols = one_gate.shape
    piece = norm_train.shape[1]
    part = cols // parts
    me, col = lax.axis_index("shard"), lax.axis_index("model")
    at = position_of(me, n)

    ones, others = (one_gate, one_up), (other_gate, other_up)
    finals, columns = (final_gate, final_up), (column_gate, column_up)

    loads = {}
    for w in range(2):
        for c in range(parts):
            span = pl.ds(c * part, part)
            pair = (
                pltpu.make_async_copy(ones[w].at[:, span], held_one.at[w, :, span], load_sem.at[w, c, 0]),
                pltpu.make_async_copy(others[w].at[:, span], held_other.at[w, :, span], load_sem.at[w, c, 1]),
            )
            for copy in pair:
                copy.start()
            loads[w, c] = pair

    barrier = pltpu.get_barrier_semaphore()
    for d in range(1, n):
        pl.semaphore_signal(barrier, inc=1, device_id=((me + d) % n, col), device_id_type=MESH)
    for d in range(1, k):
        pl.semaphore_signal(barrier, inc=1, device_id=(me, (col + d) % k), device_id_type=MESH)

    share[...] = jnp.broadcast_to(mix[...], (LANES, rows)).T

    maxima[1, parts - 1, 0, :, part:part + piece] = norm_train[...] + norm_step[...]

    def mixed(w, c):
        for copy in loads[w, c]:
            copy.wait()
        span = pl.ds(c * part, part)

        def step(g, top):
            lines = pl.ds(pl.multiple_of(g * 8, 8), 8)
            m = share[lines, 0:1]
            result = m * held_one[w, lines, span] + (1.0 - m) * held_other[w, lines, span]
            held_one[w, lines, span] = result
            return jnp.maximum(top, jnp.abs(result))

        top = lax.fori_loop(0, rows // 8, step, jnp.zeros((8, part), jnp.float32), unroll=4)
        maxima[w, c, 0, :, 0:part] = jnp.max(top, axis=0, keepdims=True)

    def tell(w, c):
        width = part + LANES if (w, c) == (1, parts - 1) else part
        copies = []
        for d in range(1, n):
            copy = pltpu.make_async_remote_copy(
                src_ref=maxima.at[w, c, 0, :, pl.ds(0, width)], dst_ref=maxima.at[w, c, d, :, pl.ds(0, width)],
                send_sem=max_send.at[w, c, d], recv_sem=max_recv.at[w, c, d],
                device_id=((me + d) % n, col), device_id_type=MESH,
            )
            copy.start()
            copies.append(copy)
        return copies

    def ring(way, hop, w, c):
        origin = index_at((at + (n - hop if way == 0 else hop)) % n, n)
        lines, span = pl.ds(pl.multiple_of(origin * rows, rows), rows), pl.ds(c * part, part)
        to = index_at((at + (1 if way == 0 else n - 1)) % n, n)
        return pltpu.make_async_remote_copy(
            src_ref=finals[w].at[lines, span], dst_ref=finals[w].at[lines, span],
            send_sem=ring_send.at[way, hop, w, c], recv_sem=ring_recv.at[way, hop, w, c],
            device_id=(to, col), device_id_type=MESH,
        )

    def scaled(w, c, inverse):
        span = pl.ds(c * part, part)

        def step(g, _):
            start = pl.multiple_of(g * 16, 16)
            to = pl.multiple_of(me * rows + g * 16, 16)
            finals[w][pl.ds(to, 16), span] = (held_one[w, pl.ds(start, 16), span] * inverse).astype(jnp.bfloat16)
            return 0

        lax.fori_loop(0, rows // 16, step, 0, unroll=2)

    units = [(w, c) for w in range(2) for c in range(parts)]
    told = {}
    for w, c in units:
        mixed(w, c)
        if (w, c) == units[0]:
            pl.semaphore_wait(barrier, n - 1 + k - 1)
        told[w, c] = tell(w, c)

    sent, norms = {}, []
    for w, c in units:
        for copy in told[w, c]:
            copy.wait_recv()
        column = jnp.max(maxima[w, c, :, :, 0:part], axis=0)
        columns[w][:, pl.ds(c * part, part)] = column
        scaled(w, c, 1.0 / column)
        for way in range(2):
            sent[way, 0, w, c] = ring(way, 0, w, c)
            sent[way, 0, w, c].start()

    for d in range(n):
        gains[0, pl.ds((me + (n - d)) % n, 1), :] = maxima[1, parts - 1, d, :, part:part + LANES]
    for d in range(1, k):
        copy = pltpu.make_async_remote_copy(
            src_ref=gains.at[0], dst_ref=gains.at[d],
            send_sem=norm_send.at[d], recv_sem=norm_recv.at[d],
            device_id=(me, (col + d) % k), device_id_type=MESH,
        )
        copy.start()
        norms.append(copy)
    for copy in norms:
        copy.wait_recv()
    gain = jnp.concatenate([gains[(col + (k - j)) % k][:, 0:piece] for j in range(k)], axis=1)
    if serve_norm.shape[1] == gain.shape[1]:
        serve_norm[...] = gain.astype(jnp.bfloat16)
    else:
        each = k * piece // LANES
        for i in range(n * each):
            at_lane = i % each * LANES
            gain_rows[i:i + 1, :] = gain[i // each:i // each + 1, at_lane:at_lane + LANES]
        serve_norm[...] = gain_rows[...].astype(jnp.bfloat16)

    for hop in range(1, n // 2 + 1):
        for w in range(2):
            for c in range(parts):
                for way in range(2):
                    if (way, hop - 1, w, c) not in sent:
                        continue
                    sent[way, hop - 1, w, c].wait_recv()
                    if hop < n // 2 - 1 or (hop == n // 2 - 1 and way == w):
                        sent[way, hop, w, c] = ring(way, hop, w, c)
                        sent[way, hop, w, c].start()

    for copy in sent.values():
        copy.wait_send()
    for copy in sum(told.values(), norms):
        copy.wait_send()


def writer(*refs):
    (sem,), count = refs[-1:], (len(refs) - 1) // 2
    copies = []
    for source, target in zip(refs[:count], refs[count:-1]):
        pieces = 4 if source.shape[0] > LANES else 1
        lines = source.shape[0] // pieces
        for p in range(pieces):
            span = pl.ds(p * lines, lines)
            copies.append(pltpu.make_async_copy(source.at[span], target.at[span], sem.at[len(copies)]))
    for copy in copies:
        copy.start()
    for copy in copies:
        copy.wait()


def solution(mesh):
    n, k = mesh.shape["shard"], mesh.shape["model"]

    def local(one_gate, other_gate, one_up, other_up, mix_share, norm_train, norm_step):
        rows, cols = one_gate.shape
        piece = norm_train.shape[0]
        parts = 2 if n <= 8 else 1
        near = n <= 8
        shaped = pltpu.VMEM if near else jax.ShapeDtypeStruct
        norm_shape = (n * k * piece // LANES, LANES) if k * piece % LANES == 0 else (n, k * piece)
        shapes = [
            ((n * rows, cols), jnp.bfloat16), ((n * rows, cols), jnp.bfloat16),
            ((1, cols), jnp.float32), ((1, cols), jnp.float32), (norm_shape, jnp.bfloat16),
        ]
        hbm, vmem = pl.BlockSpec(memory_space=pltpu.HBM), pl.BlockSpec(memory_space=pltpu.VMEM)
        results = pl.pallas_call(
            functools.partial(kernel, n, k, parts),
            out_shape=[shaped(*shape) for shape in shapes],
            in_specs=[hbm] * 4 + [vmem] * 3,
            out_specs=[vmem] * 5,
            scratch_shapes=[
                pltpu.VMEM((2, rows, cols), jnp.float32),
                pltpu.VMEM((2, rows, cols), jnp.float32),
                pltpu.VMEM((rows, LANES), jnp.float32),
                pltpu.VMEM((2, parts, n, 1, cols // parts + LANES), jnp.float32),
                pltpu.VMEM((k, n, LANES), jnp.float32),
                pltpu.VMEM((max(n * k * piece // LANES, 8), LANES), jnp.float32),
                pltpu.SemaphoreType.DMA((2, parts, 2)),
                pltpu.SemaphoreType.DMA((2, parts, n)),
                pltpu.SemaphoreType.DMA((2, parts, n)),
                pltpu.SemaphoreType.DMA((k,)),
                pltpu.SemaphoreType.DMA((k,)),
                pltpu.SemaphoreType.DMA((2, n // 2, 2, parts)),
                pltpu.SemaphoreType.DMA((2, n // 2, 2, parts)),
            ],
            compiler_params=pltpu.CompilerParams(
                collective_id=0, has_side_effects=True, vmem_limit_bytes=46 * 2**20
            ),
        )(
            one_gate, other_gate, one_up, other_up,
            mix_share.reshape(1, rows), norm_train.reshape(1, piece), norm_step.reshape(1, piece),
        )
        if near:
            results = pl.pallas_call(
                writer,
                out_shape=[jax.ShapeDtypeStruct(*shape) for shape in shapes],
                in_specs=[vmem] * 5,
                out_specs=[hbm] * 5,
                scratch_shapes=[pltpu.SemaphoreType.DMA((11,))],
                compiler_params=pltpu.CompilerParams(vmem_limit_bytes=2**20),
            )(*results)
        final_gate, final_up, column_gate, column_up, serve_norm = results
        return (
            final_gate, final_up, column_gate.reshape(cols), column_up.reshape(cols),
            serve_norm.reshape(n * k * piece),
        )

    return jax.shard_map(
        local,
        mesh=mesh,
        in_specs=(
            P("shard", "model"), P("shard", "model"), P("shard", "model"), P("shard", "model"),
            P("shard"), P(("shard", "model")), P(("shard", "model")),
        ),
        out_specs=(P(None, "model"), P(None, "model"), P("model"), P("model"), P()),
        check_vma=False,
    )
```

profile of v0, /device:TPU:0, one launch (start us, length us, event | category | flops | bytes accessed | tf_op | source)
XLA Modules:
  0.0 176.9 jit_solution(10208702115904466838)
XLA Ops:
  0.6 170.3 %shard_map.110 = (bf16[2048,2048]{1,0:T(8,128)(2,1)S(1)}, bf16[2048,2048]{1,0:T(8,128)(2,1)S(1)}, f32[1,2048]{1,0:T(1,128)S(1)}, f32[1,2048]{1,0:T(1,128)S(1)}, bf16[16,128]{1,0:T(8,128)(2,1)S(1)}) custom-call(f32[256,2048]{1,0:T(8,128)} %one_gate.1, f32[256,2048]{1,0:T(8,128)} %other_gate.1, f32[256,2048]{1,0:T(8,128)} %one_up.1, f32[256,2048]{1,0:T(8,128)} %other_up.1, ...), custom_call_target="tpu_custom_call" | custom-call | tf_op jit(solution)/shard_map/pallas_call | solution.py:197
  171.0 6.0 %shard_map.111 = (bf16[2048,2048]{1,0:T(8,128)(2,1)}, bf16[2048,2048]{1,0:T(8,128)(2,1)}, f32[1,2048]{1,0:T(1,128)}, f32[1,2048]{1,0:T(1,128)}, bf16[16,128]{1,0:T(8,128)(2,1)}) custom-call(bf16[2048,2048]{1,0:T(8,128)(2,1)S(1)} %get-tuple-element.15.refs_0_, bf16[2048,2048]{1,0:T(8,128)(2,1)S(1)} %get-tuple-element.16.refs_1_, ...), custom_call_target="tpu_custom_call" | custom-call | tf_op jit(solution)/shard_map/pallas_call | solution.py:225
where the time goes:
time: 177 us
  Pallas kernels  176 us (99%)
    pallas_call x1, Pallas kernels, local(): pl.pallas_call(functools.partial(kernel, n, k, parts), out_shape=[shaped(...  170 us
    pallas_call x1, Pallas kernels, local(): pl.pallas_call(writer, out_shape=[jax.ShapeDtypeStruct(*shape) for shape...  5.96 us

commit v1 on v0

--- a/solution.py
+++ b/solution.py
@@ -164,6 +164,204 @@
         copy.wait_send()
 
 
+def near_kernel(
+    n, k, units, early,
+    one_gate, other_gate, one_up, other_up, mix, norm_train, norm_step,
+    final_gate, final_up, column_gate, column_up, serve_norm,
+    held_one, held_other, mix_held, train_held, step_held, share, raw, maxima, gains, gain_rows,
+    load_sem, small_sem, raw_send, raw_recv, max_send, max_recv, norm_send, norm_recv, ring_send, ring_recv,
+):
+    rows, cols = one_gate.shape
+    piece = norm_train.shape[1]
+    me, col = lax.axis_index("shard"), lax.axis_index("model")
+    at = position_of(me, n)
+
+    ones, others = (one_gate, one_up), (other_gate, other_up)
+    finals, columns = (final_gate, final_up), (column_gate, column_up)
+
+    smalls = (
+        pltpu.make_async_copy(mix, mix_held, small_sem.at[0]),
+        pltpu.make_async_copy(norm_train, train_held, small_sem.at[1]),
+        pltpu.make_async_copy(norm_step, step_held, small_sem.at[2]),
+    )
+    smalls[0].start()
+
+    loads = {}
+
+    def load(u):
+        w, first, width = units[u]
+        span = pl.ds(first, width)
+        loads[u] = (
+            pltpu.make_async_copy(ones[w].at[:, span], held_one.at[w, :, span], load_sem.at[u, 0]),
+            pltpu.make_async_copy(others[w].at[:, span], held_other.at[w, :, span], load_sem.at[u, 1]),
+        )
+        for copy in loads[u]:
+            copy.start()
+
+    load(0)
+    barrier = pltpu.get_barrier_semaphore()
+    for d in range(n - 1, 0, -1):
+        pl.semaphore_signal(barrier, inc=1, device_id=((me + d) % n, col), device_id_type=MESH)
+    for d in range(1, k):
+        pl.semaphore_signal(barrier, inc=1, device_id=(me, (col + d) % k), device_id_type=MESH)
+    load(early)
+    for u in range(1, len(units)):
+        if u != early:
+            load(u)
+    for copy in smalls[1:]:
+        copy.start()
+
+    smalls[0].wait()
+    share[...] = jnp.broadcast_to(mix_held[...], (LANES, rows)).T
+
+    def mixed(u):
+        for copy in loads[u]:
+            copy.wait()
+        w, first, width = units[u]
+        span = pl.ds(first, width)
+
+        def step(g, top):
+            lines = pl.ds(pl.multiple_of(g * 8, 8), 8)
+            m = share[lines, :]
+            both = jnp.concatenate([m] * (width // LANES), axis=1)
+            rest = jnp.concatenate([1.0 - m] * (width // LANES), axis=1)
+            result = both * held_one[w, lines, span] + rest * held_other[w, lines, span]
+            held_one[w, lines, span] = result
+            return jnp.maximum(top, jnp.abs(result))
+
+        top = lax.fori_loop(0, rows // 8, step, jnp.zeros((8, width), jnp.float32), unroll=4)
+        maxima[w, 0, :, span] = jnp.max(top, axis=0, keepdims=True)
+
+    def tell(u):
+        w, first, width = units[u]
+        span = pl.ds(first, width + LANES if u == early else width)
+        copies = []
+        for d in range(1, n):
+            copy = pltpu.make_async_remote_copy(
+                src_ref=maxima.at[w, 0, :, span], dst_ref=maxima.at[w, d, :, span],
+                send_sem=max_send.at[u, d], recv_sem=max_recv.at[u, d],
+                device_id=((me + d) % n, col), device_id_type=MESH,
+            )
+            copy.start()
+            copies.append(copy)
+        return copies
+
+    def toward(way):
+        return index_at((at + (1 if way == 0 else n - 1)) % n, n)
+
+    def origin_of(way, hop):
+        return index_at((at + (n - hop if way == 0 else hop)) % n, n)
+
+    def ring(way, hop, u):
+        w, first, width = units[u]
+        lines = pl.ds(pl.multiple_of(origin_of(way, hop) * rows, rows), rows)
+        span = pl.ds(first, width)
+        return pltpu.make_async_remote_copy(
+            src_ref=finals[w].at[lines, span], dst_ref=finals[w].at[lines, span],
+            send_sem=ring_send.at[way, hop, u], recv_sem=ring_recv.at[way, hop, u],
+            device_id=(toward(way), col), device_id_type=MESH,
+        )
+
+    def ahead(way):
+        w, first, width = units[early]
+        return pltpu.make_async_remote_copy(
+            src_ref=held_one.at[w, :, pl.ds(first, width)], dst_ref=raw.at[way],
+            send_sem=raw_send.at[way], recv_sem=raw_recv.at[way],
+            device_id=(toward(way), col), device_id_type=MESH,
+        )
+
+    def scaled(u, origin, inverse, read):
+        w, first, width = units[u]
+
+        def step(g, _):
+            start = pl.multiple_of(g * 16, 16)
+            to = pl.multiple_of(origin * rows + g * 16, 16)
+            finals[w][pl.ds(to, 16), pl.ds(first, width)] = (read(pl.ds(start, 16)) * inverse).astype(jnp.bfloat16)
+            return 0
+
+        lax.fori_loop(0, rows // 16, step, 0, unroll=2)
+
+    def scale_of(u):
+        for copy in told[u]:
+            copy.wait_recv()
+        w, first, width = units[u]
+        span = pl.ds(first, width)
+        column = jnp.max(maxima[w, :, :, span], axis=0)
+        columns[w][:, span] = column
+        return 1.0 / column
+
+    told, sent, norms = {}, {}, []
+    mixed(0)
+    pl.semaphore_wait(barrier, n - 1 + k - 1)
+    told[0] = tell(0)
+    mixed(early)
+    aheads = [ahead(way) for way in range(2)]
+    for copy in aheads:
+        copy.start()
+    for copy in smalls[1:]:
+        copy.wait()
+    maxima[units[early][0], 0, :, cols:cols + piece] = train_held[...] + step_held[...]
+    for u in range(1, len(units)):
+        if u != early:
+            mixed(u)
+        told[u] = tell(u)
+
+    order = [u for u in range(len(units)) if u != early]
+    for u in order:
+        w, first, width = units[u]
+        inverse = scale_of(u)
+        scaled(u, me, inverse, lambda lines: held_one[w, lines, pl.ds(first, width)])
+        for way in range(2):
+            sent[way, 0, u] = ring(way, 0, u)
+            sent[way, 0, u].start()
+
+    w, first, width = units[early]
+    inverse = scale_of(early)
+    for way in range(2):
+        aheads[way].wait_recv()
+        scaled(early, origin_of(way, 1), inverse, lambda lines: raw[way, lines, :])
+        sent[way, 1, early] = ring(way, 1, early)
+        sent[way, 1, early].start()
+    scaled(early, me, inverse, lambda lines: held_one[w, lines, pl.ds(first, width)])
+
+    for d in range(n):
+        gains[0, pl.ds((me + (n - d)) % n, 1), :] = maxima[units[early][0], d, :, cols:cols + LANES]
+    for d in range(1, k):
+        copy = pltpu.make_async_remote_copy(
+            src_ref=gains.at[0], dst_ref=gains.at[d],
+            send_sem=norm_send.at[d], recv_sem=norm_recv.at[d],
+            device_id=(me, (col + d) % k), device_id_type=MESH,
+        )
+        copy.start()
+        norms.append(copy)
+    for copy in norms:
+        copy.wait_recv()
+    gain = jnp.concatenate([gains[(col + (k - j)) % k][:, 0:piece] for j in range(k)], axis=1)
+    if serve_norm.shape[1] == gain.shape[1]:
+        serve_norm[...] = gain.astype(jnp.bfloat16)
+    else:
+        each = k * piece // LANES
+        for i in range(n * each):
+            at_lane = i % each * LANES
+            gain_rows[i:i + 1, :] = gain[i // each:i // each + 1, at_lane:at_lane + LANES]
+        serve_norm[...] = gain_rows[...].astype(jnp.bfloat16)
+
+    for hop in range(1, n // 2 + 1):
+        for u in order + [early]:
+            for way in range(2):
+                if (way, hop - 1, u) not in sent:
+                    continue
+                sent[way, hop - 1, u].wait_recv()
+                if hop < n // 2 - 1 or (hop == n // 2 - 1 and way == units[u][0]):
+                    sent[way, hop, u] = ring(way, hop, u)
+                    sent[way, hop, u].start()
+
+    for copy in list(sent.values()) + aheads:
+        copy.wait_send()
+    for copy in sum(told.values(), norms):
+        copy.wait_send()
+
+
 def writer(*refs):
     (sem,), count = refs[-1:], (len(refs) - 1) // 2
     copies = []
@@ -194,26 +392,47 @@
             ((1, cols), jnp.float32), ((1, cols), jnp.float32), (norm_shape, jnp.bfloat16),
         ]
         hbm, vmem = pl.BlockSpec(memory_space=pltpu.HBM), pl.BlockSpec(memory_space=pltpu.VMEM)
-        results = pl.pallas_call(
-            functools.partial(kernel, n, k, parts),
-            out_shape=[shaped(*shape) for shape in shapes],
-            in_specs=[hbm] * 4 + [vmem] * 3,
-            out_specs=[vmem] * 5,
-            scratch_shapes=[
-                pltpu.VMEM((2, rows, cols), jnp.float32),
-                pltpu.VMEM((2, rows, cols), jnp.float32),
+        e = cols // 8
+        units = ((0, 0, 2 * e), (0, 2 * e, 2 * e), (0, 4 * e, 4 * e), (1, 0, 4 * e), (1, 4 * e, 3 * e), (1, 7 * e, e))
+        early = len(units) - 1
+        common = [
+            pltpu.VMEM((2, rows, cols), jnp.float32),
+            pltpu.VMEM((2, rows, cols), jnp.float32),
+        ]
+        gain_shapes = [
+            pltpu.VMEM((k, n, LANES), jnp.float32),
+            pltpu.VMEM((max(n * k * piece // LANES, 8), LANES), jnp.float32),
+        ]
+        sems = pltpu.SemaphoreType.DMA
+        if near:
+            body = functools.partial(near_kernel, n, k, units, early)
+            small_spec = hbm
+            scratch = common + [
+                pltpu.VMEM((1, rows), jnp.float32), pltpu.VMEM((1, piece), jnp.float32), pltpu.VMEM((1, piece), jnp.float32),
+                pltpu.VMEM((rows, LANES), jnp.float32),
+                pltpu.VMEM((2, rows, e), jnp.float32),
+                pltpu.VMEM((2, n, 1, cols + LANES), jnp.float32),
+            ] + gain_shapes + [
+                sems((len(units), 2)), sems((3,)), sems((2,)), sems((2,)),
+                sems((len(units), n)), sems((len(units), n)), sems((k,)), sems((k,)),
+                sems((2, n // 2, len(units))), sems((2, n // 2, len(units))),
+            ]
+        else:
+            body = functools.partial(kernel, n, k, parts)
+            small_spec = vmem
+            scratch = common + [
                 pltpu.VMEM((rows, LANES), jnp.float32),
                 pltpu.VMEM((2, parts, n, 1, cols // parts + LANES), jnp.float32),
-                pltpu.VMEM((k, n, LANES), jnp.float32),
-                pltpu.VMEM((max(n * k * piece // LANES, 8), LANES), jnp.float32),
-                pltpu.SemaphoreType.DMA((2, parts, 2)),
-                pltpu.SemaphoreType.DMA((2, parts, n)),
-                pltpu.SemaphoreType.DMA((2, parts, n)),
-                pltpu.SemaphoreType.DMA((k,)),
-                pltpu.SemaphoreType.DMA((k,)),
-                pltpu.SemaphoreType.DMA((2, n // 2, 2, parts)),
-                pltpu.SemaphoreType.DMA((2, n // 2, 2, parts)),
-            ],
+            ] + gain_shapes + [
+                sems((2, parts, 2)), sems((2, parts, n)), sems((2, parts, n)), sems((k,)), sems((k,)),
+                sems((2, n // 2, 2, parts)), sems((2, n // 2, 2, parts)),
+            ]
+        results = pl.pallas_call(
+            body,
+            out_shape=[shaped(*shape) for shape in shapes],
+            in_specs=[hbm] * 4 + [small_spec] * 3,
+            out_specs=[vmem] * 5,
+            scratch_shapes=scratch,
             compiler_params=pltpu.CompilerParams(
                 collective_id=0, has_side_effects=True, vmem_limit_bytes=46 * 2**20
             ),

time: 177 us -> 178 us (level)
  no operation moved by 1% of the time
where the time goes in v1:
time: 178 us
  Pallas kernels  177 us (99%)
    pallas_call x1, Pallas kernels, local(): pl.pallas_call(body, out_shape=[shaped(*shape) for shape in shapes], in_s...  172 us
    pallas_call x1, Pallas kernels, local(): pl.pallas_call(writer, out_shape=[jax.ShapeDtypeStruct(*shape) for shape...  5.96 us

profile of v1, /device:TPU:0, one launch (start us, length us, event | category | flops | bytes accessed | tf_op | source)
XLA Modules:
  0.0 178.1 jit_solution(5150823250080486953)
XLA Ops:
  0.6 171.5 %shard_map.110 = (bf16[2048,2048]{1,0:T(8,128)(2,1)S(1)}, bf16[2048,2048]{1,0:T(8,128)(2,1)S(1)}, f32[1,2048]{1,0:T(1,128)S(1)}, f32[1,2048]{1,0:T(1,128)S(1)}, bf16[16,128]{1,0:T(8,128)(2,1)S(1)}) custom-call(f32[256,2048]{1,0:T(8,128)} %one_gate.1, f32[256,2048]{1,0:T(8,128)} %other_gate.1, f32[256,2048]{1,0:T(8,128)} %one_up.1, f32[256,2048]{1,0:T(8,128)} %other_up.1, ...), custom_call_target="tpu_custom_call" | custom-call | tf_op jit(solution)/shard_map/pallas_call | solution.py:430
  172.2 6.0 %shard_map.111 = (bf16[2048,2048]{1,0:T(8,128)(2,1)}, bf16[2048,2048]{1,0:T(8,128)(2,1)}, f32[1,2048]{1,0:T(1,128)}, f32[1,2048]{1,0:T(1,128)}, bf16[16,128]{1,0:T(8,128)(2,1)}) custom-call(bf16[2048,2048]{1,0:T(8,128)(2,1)S(1)} %get-tuple-element.15.refs_0_, bf16[2048,2048]{1,0:T(8,128)(2,1)S(1)} %get-tuple-element.16.refs_1_, ...), custom_call_target="tpu_custom_call" | custom-call | tf_op jit(solution)/shard_map/pallas_call | solution.py:444

commit v2 on v1

--- a/solution.py
+++ b/solution.py
@@ -165,27 +165,30 @@
 
 
 def near_kernel(
-    n, k, units, early,
+    n, k, units, direct, early,
     one_gate, other_gate, one_up, other_up, mix, norm_train, norm_step,
     final_gate, final_up, column_gate, column_up, serve_norm,
-    held_one, held_other, mix_held, train_held, step_held, share, raw, maxima, gains, gain_rows,
-    load_sem, small_sem, raw_send, raw_recv, max_send, max_recv, norm_send, norm_recv, ring_send, ring_recv,
+    held_one, held_other, result, mix_held, train_held, step_held, share, raw, mine, heard, partial, whole, gains, gain_rows,
+    load_sem, small_sem, raw_send, raw_recv, max_send, max_recv, part_send, part_recv, whole_send, whole_recv,
+    norm_send, norm_recv, ring_send, ring_recv,
 ):
     rows, cols = one_gate.shape
     piece = norm_train.shape[1]
+    block = mine.shape[2]
     me, col = lax.axis_index("shard"), lax.axis_index("model")
     at = position_of(me, n)
 
     ones, others = (one_gate, one_up), (other_gate, other_up)
     finals, columns = (final_gate, final_up), (column_gate, column_up)
+
+    def peer(d):
+        return ((me + d) % n, col)
 
     smalls = (
         pltpu.make_async_copy(mix, mix_held, small_sem.at[0]),
         pltpu.make_async_copy(norm_train, train_held, small_sem.at[1]),
         pltpu.make_async_copy(norm_step, step_held, small_sem.at[2]),
     )
-    smalls[0].start()
-
     loads = {}
 
     def load(u):
@@ -198,16 +201,16 @@
         for copy in loads[u]:
             copy.start()
 
+    smalls[0].start()
     load(0)
     barrier = pltpu.get_barrier_semaphore()
-    for d in range(n - 1, 0, -1):
-        pl.semaphore_signal(barrier, inc=1, device_id=((me + d) % n, col), device_id_type=MESH)
+    for d in range(1, n):
+        pl.semaphore_signal(barrier, inc=1, device_id=peer(d), device_id_type=MESH)
     for d in range(1, k):
         pl.semaphore_signal(barrier, inc=1, device_id=(me, (col + d) % k), device_id_type=MESH)
     load(early)
-    for u in range(1, len(units)):
-        if u != early:
-            load(u)
+    for u in range(1, early):
+        load(u)
     for copy in smalls[1:]:
         copy.start()
 
@@ -225,22 +228,25 @@
             m = share[lines, :]
             both = jnp.concatenate([m] * (width // LANES), axis=1)
             rest = jnp.concatenate([1.0 - m] * (width // LANES), axis=1)
-            result = both * held_one[w, lines, span] + rest * held_other[w, lines, span]
-            held_one[w, lines, span] = result
-            return jnp.maximum(top, jnp.abs(result))
+            value = both * held_one[w, lines, span] + rest * held_other[w, lines, span]
+            result[w, lines, span] = value
+            return jnp.maximum(top, jnp.abs(value))
 
         top = lax.fori_loop(0, rows // 8, step, jnp.zeros((8, width), jnp.float32), unroll=4)
-        maxima[w, 0, :, span] = jnp.max(top, axis=0, keepdims=True)
+        top = jnp.max(top, axis=0, keepdims=True)
+        done = 0
+        while done < width:
+            b, lane = (w * cols + first + done) // block, (first + done) % block
+            take = min(block - lane, width - done)
+            mine[b, :, lane:lane + take] = top[:, done:done + take]
+            done += take
 
     def tell(u):
-        w, first, width = units[u]
-        span = pl.ds(first, width + LANES if u == early else width)
         copies = []
         for d in range(1, n):
             copy = pltpu.make_async_remote_copy(
-                src_ref=maxima.at[w, 0, :, span], dst_ref=maxima.at[w, d, :, span],
-                send_sem=max_send.at[u, d], recv_sem=max_recv.at[u, d],
-                device_id=((me + d) % n, col), device_id_type=MESH,
+                src_ref=mine.at[u], dst_ref=heard.at[u, d],
+                send_sem=max_send.at[u, d], recv_sem=max_recv.at[u, d], device_id=peer(d), device_id_type=MESH,
             )
             copy.start()
             copies.append(copy)
@@ -265,7 +271,7 @@
     def ahead(way):
         w, first, width = units[early]
         return pltpu.make_async_remote_copy(
-            src_ref=held_one.at[w, :, pl.ds(first, width)], dst_ref=raw.at[way],
+            src_ref=result.at[w, :, pl.ds(first, width)], dst_ref=raw.at[way],
             send_sem=raw_send.at[way], recv_sem=raw_recv.at[way],
             device_id=(toward(way), col), device_id_type=MESH,
         )
@@ -281,16 +287,26 @@
 
         lax.fori_loop(0, rows // 16, step, 0, unroll=2)
 
-    def scale_of(u):
+    def held(u):
+        w, first, width = units[u]
+        return lambda lines: result[w, lines, pl.ds(first, width)]
+
+    sent, told = {}, {}
+
+    def begin(u, inverse):
+        scaled(u, me, inverse, held(u))
+        for way in range(2):
+            sent[way, 0, u] = ring(way, 0, u)
+            sent[way, 0, u].start()
+
+    def heard_of(u):
         for copy in told[u]:
             copy.wait_recv()
-        w, first, width = units[u]
-        span = pl.ds(first, width)
-        column = jnp.max(maxima[w, :, :, span], axis=0)
-        columns[w][:, span] = column
-        return 1.0 / column
-
-    told, sent, norms = {}, {}, []
+        top = mine[u]
+        for d in range(1, n):
+            top = jnp.maximum(top, heard[u, d])
+        return 1.0 / top
+
     mixed(0)
     pl.semaphore_wait(barrier, n - 1 + k - 1)
     told[0] = tell(0)
@@ -298,34 +314,69 @@
     aheads = [ahead(way) for way in range(2)]
     for copy in aheads:
         copy.start()
+    for u in range(1, direct):
+        mixed(u)
+        told[u] = tell(u)
+    for u in range(direct, early):
+        mixed(u)
+
+    parts = []
+    for d in range(1, n):
+        copy = pltpu.make_async_remote_copy(
+            src_ref=mine.at[(me + d) % n], dst_ref=partial.at[d],
+            send_sem=part_send.at[d], recv_sem=part_recv.at[d], device_id=peer(d), device_id_type=MESH,
+        )
+        copy.start()
+        parts.append(copy)
+
     for copy in smalls[1:]:
         copy.wait()
-    maxima[units[early][0], 0, :, cols:cols + piece] = train_held[...] + step_held[...]
-    for u in range(1, len(units)):
-        if u != early:
-            mixed(u)
-        told[u] = tell(u)
-
-    order = [u for u in range(len(units)) if u != early]
-    for u in order:
+    begin(0, heard_of(0))
+
+    for copy in parts:
+        copy.wait_recv()
+    top = mine[me]
+    for d in range(1, n):
+        top = jnp.maximum(top, partial[d])
+    whole[me, :, 0:block] = top
+    whole[me, :, block:block + piece] = train_held[...] + step_held[...]
+    wholes = []
+    for d in range(1, n):
+        copy = pltpu.make_async_remote_copy(
+            src_ref=whole.at[me], dst_ref=whole.at[me],
+            send_sem=whole_send.at[d], recv_sem=whole_recv.at[d], device_id=peer(d), device_id_type=MESH,
+        )
+        copy.start()
+        wholes.append(copy)
+
+    for u in range(1, direct):
+        begin(u, heard_of(u))
+
+    for d in range(1, n):
+        pltpu.make_async_remote_copy(
+            src_ref=whole.at[me], dst_ref=whole.at[(me + (n - d)) % n],
+            send_sem=whole_send.at[d], recv_sem=whole_recv.at[d], device_id=peer(d), device_id_type=MESH,
+        ).wait_recv()
+    for b in range(n):
+        w, first = b * block // cols, b * block % cols
+        columns[w][:, first:first + block] = whole[b, :, 0:block]
+
+    for u in range(direct, early):
         w, first, width = units[u]
-        inverse = scale_of(u)
-        scaled(u, me, inverse, lambda lines: held_one[w, lines, pl.ds(first, width)])
-        for way in range(2):
-            sent[way, 0, u] = ring(way, 0, u)
-            sent[way, 0, u].start()
+        begin(u, 1.0 / columns[w][:, first:first + width])
 
     w, first, width = units[early]
-    inverse = scale_of(early)
+    inverse = 1.0 / columns[w][:, first:first + width]
     for way in range(2):
         aheads[way].wait_recv()
         scaled(early, origin_of(way, 1), inverse, lambda lines: raw[way, lines, :])
         sent[way, 1, early] = ring(way, 1, early)
         sent[way, 1, early].start()
-    scaled(early, me, inverse, lambda lines: held_one[w, lines, pl.ds(first, width)])
-
+    scaled(early, me, inverse, held(early))
+
+    norms = []
     for d in range(n):
-        gains[0, pl.ds((me + (n - d)) % n, 1), :] = maxima[units[early][0], d, :, cols:cols + LANES]
+        gains[0, d:d + 1, :] = whole[d, :, block:block + LANES]
     for d in range(1, k):
         copy = pltpu.make_async_remote_copy(
             src_ref=gains.at[0], dst_ref=gains.at[d],
@@ -347,7 +398,7 @@
         serve_norm[...] = gain_rows[...].astype(jnp.bfloat16)
 
     for hop in range(1, n // 2 + 1):
-        for u in order + [early]:
+        for u in range(len(units)):
             for way in range(2):
                 if (way, hop - 1, u) not in sent:
                     continue
@@ -358,7 +409,7 @@
 
     for copy in list(sent.values()) + aheads:
         copy.wait_send()
-    for copy in sum(told.values(), norms):
+    for copy in sum(told.values(), norms + parts + wholes):
         copy.wait_send()
 
 
@@ -392,35 +443,39 @@
             ((1, cols), jnp.float32), ((1, cols), jnp.float32), (norm_shape, jnp.bfloat16),
         ]
         hbm, vmem = pl.BlockSpec(memory_space=pltpu.HBM), pl.BlockSpec(memory_space=pltpu.VMEM)
-        e = cols // 8
-        units = ((0, 0, 2 * e), (0, 2 * e, 2 * e), (0, 4 * e, 4 * e), (1, 0, 4 * e), (1, 4 * e, 3 * e), (1, 7 * e, e))
-        early = len(units) - 1
-        common = [
-            pltpu.VMEM((2, rows, cols), jnp.float32),
-            pltpu.VMEM((2, rows, cols), jnp.float32),
-        ]
+        block = 2 * cols // n
+        e = cols // 16
+        units = (
+            (0, 0, block), (0, block, block), (0, 2 * block, cols - 2 * block),
+            (1, 0, 8 * e), (1, 8 * e, 7 * e), (1, 15 * e, e),
+        )
+        direct, early = 2, len(units) - 1
         gain_shapes = [
             pltpu.VMEM((k, n, LANES), jnp.float32),
             pltpu.VMEM((max(n * k * piece // LANES, 8), LANES), jnp.float32),
         ]
         sems = pltpu.SemaphoreType.DMA
         if near:
-            body = functools.partial(near_kernel, n, k, units, early)
+            body = functools.partial(near_kernel, n, k, units, direct, early)
             small_spec = hbm
-            scratch = common + [
+            scratch = [pltpu.VMEM((2, rows, cols), jnp.float32)] * 3 + [
                 pltpu.VMEM((1, rows), jnp.float32), pltpu.VMEM((1, piece), jnp.float32), pltpu.VMEM((1, piece), jnp.float32),
                 pltpu.VMEM((rows, LANES), jnp.float32),
                 pltpu.VMEM((2, rows, e), jnp.float32),
-                pltpu.VMEM((2, n, 1, cols + LANES), jnp.float32),
+                pltpu.VMEM((n, 1, block), jnp.float32),
+                pltpu.VMEM((direct, n, 1, block), jnp.float32),
+                pltpu.VMEM((n, 1, block), jnp.float32),
+                pltpu.VMEM((n, 1, block + LANES), jnp.float32),
             ] + gain_shapes + [
                 sems((len(units), 2)), sems((3,)), sems((2,)), sems((2,)),
-                sems((len(units), n)), sems((len(units), n)), sems((k,)), sems((k,)),
+                sems((direct, n)), sems((direct, n)), sems((n,)), sems((n,)), sems((n,)), sems((n,)),
+                sems((k,)), sems((k,)),
                 sems((2, n // 2, len(units))), sems((2, n // 2, len(units))),
             ]
         else:
             body = functools.partial(kernel, n, k, parts)
             small_spec = vmem
-            scratch = common + [
+            scratch = [pltpu.VMEM((2, rows, cols), jnp.float32)] * 2 + [
                 pltpu.VMEM((rows, LANES), jnp.float32),
                 pltpu.VMEM((2, parts, n, 1, cols // parts + LANES), jnp.float32),
             ] + gain_shapes + [

time: 178 us -> 175 us (0.983)
  Pallas kernels: 177 us -> 175 us
    pallas_call x1, Pallas kernels: 172 us -> 169 us  [local(): pl.pallas_call(body, out_shape=[shaped(*shape) for shape in shapes], in_s...]
where the time goes in v2:
time: 175 us
  Pallas kernels  175 us (100%)
    pallas_call x1, Pallas kernels, local(): pl.pallas_call(body, out_shape=[shaped(*shape) for shape in shapes], in_s...  169 us
    pallas_call x1, Pallas kernels, local(): pl.pallas_call(writer, out_shape=[jax.ShapeDtypeStruct(*shape) for shape...  5.96 us

profile of v2, /device:TPU:0, one launch (start us, length us, event | category | flops | bytes accessed | tf_op | source)
XLA Modules:
  0.0 175.3 jit_solution(12499114032144606240)
XLA Ops:
  0.6 168.7 %shard_map.110 = (bf16[2048,2048]{1,0:T(8,128)(2,1)S(1)}, bf16[2048,2048]{1,0:T(8,128)(2,1)S(1)}, f32[1,2048]{1,0:T(1,128)S(1)}, f32[1,2048]{1,0:T(1,128)S(1)}, bf16[16,128]{1,0:T(8,128)(2,1)S(1)}) custom-call(f32[256,2048]{1,0:T(8,128)} %one_gate.1, f32[256,2048]{1,0:T(8,128)} %other_gate.1, f32[256,2048]{1,0:T(8,128)} %one_up.1, f32[256,2048]{1,0:T(8,128)} %other_up.1, ...), custom_call_target="tpu_custom_call" | custom-call | tf_op jit(solution)/shard_map/pallas_call | solution.py:485
  169.3 6.0 %shard_map.111 = (bf16[2048,2048]{1,0:T(8,128)(2,1)}, bf16[2048,2048]{1,0:T(8,128)(2,1)}, f32[1,2048]{1,0:T(1,128)}, f32[1,2048]{1,0:T(1,128)}, bf16[16,128]{1,0:T(8,128)(2,1)}) custom-call(bf16[2048,2048]{1,0:T(8,128)(2,1)S(1)} %get-tuple-element.15.refs_0_, bf16[2048,2048]{1,0:T(8,128)(2,1)S(1)} %get-tuple-element.16.refs_1_, ...), custom_call_target="tpu_custom_call" | custom-call | tf_op jit(solution)/shard_map/pallas_call | solution.py:499

commit v3 on v2

--- a/solution.py
+++ b/solution.py
@@ -168,9 +168,8 @@
     n, k, units, direct, early,
     one_gate, other_gate, one_up, other_up, mix, norm_train, norm_step,
     final_gate, final_up, column_gate, column_up, serve_norm,
-    held_one, held_other, result, mix_held, train_held, step_held, share, raw, mine, heard, partial, whole, gains, gain_rows,
-    load_sem, small_sem, raw_send, raw_recv, max_send, max_recv, part_send, part_recv, whole_send, whole_recv,
-    norm_send, norm_recv, ring_send, ring_recv,
+    taken, result, mix_held, norm_held, share, raw, mine, heard, partial, whole, gains, gain_rows,
+    load_sem, small_sem, raw_sem, max_send, max_recv, part_sem, whole_sem, norm_sem, ring_send, ring_recv,
 ):
     rows, cols = one_gate.shape
     piece = norm_train.shape[1]
@@ -184,24 +183,16 @@
     def peer(d):
         return ((me + d) % n, col)
 
-    smalls = (
-        pltpu.make_async_copy(mix, mix_held, small_sem.at[0]),
-        pltpu.make_async_copy(norm_train, train_held, small_sem.at[1]),
-        pltpu.make_async_copy(norm_step, step_held, small_sem.at[2]),
-    )
-    loads = {}
+    def wait_for(ref, sem):
+        pltpu.make_async_copy(ref, ref, sem).wait()
 
     def load(u):
         w, first, width = units[u]
         span = pl.ds(first, width)
-        loads[u] = (
-            pltpu.make_async_copy(ones[w].at[:, span], held_one.at[w, :, span], load_sem.at[u, 0]),
-            pltpu.make_async_copy(others[w].at[:, span], held_other.at[w, :, span], load_sem.at[u, 1]),
-        )
-        for copy in loads[u]:
-            copy.start()
-
-    smalls[0].start()
+        for i, source in enumerate((ones[w], others[w])):
+            pltpu.make_async_copy(source.at[:, span], taken.at[w, i, :, span], load_sem.at[u]).start()
+
+    pltpu.make_async_copy(mix, mix_held, small_sem.at[0]).start()
     load(0)
     barrier = pltpu.get_barrier_semaphore()
     for d in range(1, n):
@@ -211,24 +202,23 @@
     load(early)
     for u in range(1, early):
         load(u)
-    for copy in smalls[1:]:
-        copy.start()
-
-    smalls[0].wait()
+    for i, source in enumerate((norm_train, norm_step)):
+        pltpu.make_async_copy(source, norm_held.at[i], small_sem.at[1]).start()
+
+    wait_for(mix_held, small_sem.at[0])
     share[...] = jnp.broadcast_to(mix_held[...], (LANES, rows)).T
 
     def mixed(u):
-        for copy in loads[u]:
-            copy.wait()
         w, first, width = units[u]
         span = pl.ds(first, width)
+        wait_for(taken.at[w, :, :, span], load_sem.at[u])
 
         def step(g, top):
             lines = pl.ds(pl.multiple_of(g * 8, 8), 8)
             m = share[lines, :]
             both = jnp.concatenate([m] * (width // LANES), axis=1)
             rest = jnp.concatenate([1.0 - m] * (width // LANES), axis=1)
-            value = both * held_one[w, lines, span] + rest * held_other[w, lines, span]
+            value = both * taken[w, 0, lines, span] + rest * taken[w, 1, lines, span]
             result[w, lines, span] = value
             return jnp.maximum(top, jnp.abs(value))
 
@@ -242,15 +232,18 @@
             done += take
 
     def tell(u):
-        copies = []
         for d in range(1, n):
-            copy = pltpu.make_async_remote_copy(
+            pltpu.make_async_remote_copy(
                 src_ref=mine.at[u], dst_ref=heard.at[u, d],
-                send_sem=max_send.at[u, d], recv_sem=max_recv.at[u, d], device_id=peer(d), device_id_type=MESH,
-            )
-            copy.start()
-            copies.append(copy)
-        return copies
+                send_sem=max_send.at[0], recv_sem=max_recv.at[u], device_id=peer(d), device_id_type=MESH,
+            ).start()
+
+    def heard_of(u):
+        wait_for(heard.at[u, pl.ds(1, n - 1)], max_recv.at[u])
+        top = mine[u]
+        for d in range(1, n):
+            top = jnp.maximum(top, heard[u, d])
+        return 1.0 / top
 
     def toward(way):
         return index_at((at + (1 if way == 0 else n - 1)) % n, n)
@@ -258,23 +251,17 @@
     def origin_of(way, hop):
         return index_at((at + (n - hop if way == 0 else hop)) % n, n)
 
-    def ring(way, hop, u):
-        w, first, width = units[u]
-        lines = pl.ds(pl.multiple_of(origin_of(way, hop) * rows, rows), rows)
-        span = pl.ds(first, width)
-        return pltpu.make_async_remote_copy(
-            src_ref=finals[w].at[lines, span], dst_ref=finals[w].at[lines, span],
-            send_sem=ring_send.at[way, hop, u], recv_sem=ring_recv.at[way, hop, u],
+    def place(origin, w, first, width):
+        return finals[w].at[pl.ds(pl.multiple_of(origin * rows, rows), rows), pl.ds(first, width)]
+
+    def send(way, hop, w, first, width, send_sem, recv_sem):
+        part = place(origin_of(way, hop), w, first, width)
+        pltpu.make_async_remote_copy(
+            src_ref=part, dst_ref=part, send_sem=send_sem, recv_sem=recv_sem,
             device_id=(toward(way), col), device_id_type=MESH,
-        )
-
-    def ahead(way):
-        w, first, width = units[early]
-        return pltpu.make_async_remote_copy(
-            src_ref=result.at[w, :, pl.ds(first, width)], dst_ref=raw.at[way],
-            send_sem=raw_send.at[way], recv_sem=raw_recv.at[way],
-            device_id=(toward(way), col), device_id_type=MESH,
-        )
+        ).start()
+
+    e_weight, e_first, e_width = units[early]
 
     def scaled(u, origin, inverse, read):
         w, first, width = units[u]
@@ -291,72 +278,50 @@
         w, first, width = units[u]
         return lambda lines: result[w, lines, pl.ds(first, width)]
 
-    sent, told = {}, {}
-
     def begin(u, inverse):
         scaled(u, me, inverse, held(u))
         for way in range(2):
-            sent[way, 0, u] = ring(way, 0, u)
-            sent[way, 0, u].start()
-
-    def heard_of(u):
-        for copy in told[u]:
-            copy.wait_recv()
-        top = mine[u]
-        for d in range(1, n):
-            top = jnp.maximum(top, heard[u, d])
-        return 1.0 / top
+            send(way, 0, *units[u], ring_send.at[way, units[u][0]], ring_recv.at[0, way, units[u][0]])
 
     mixed(0)
     pl.semaphore_wait(barrier, n - 1 + k - 1)
-    told[0] = tell(0)
+    tell(0)
     mixed(early)
-    aheads = [ahead(way) for way in range(2)]
-    for copy in aheads:
-        copy.start()
+    for way in range(2):
+        pltpu.make_async_remote_copy(
+            src_ref=result.at[e_weight, :, pl.ds(e_first, e_width)], dst_ref=raw.at[way],
+            send_sem=raw_sem.at[0], recv_sem=raw_sem.at[1], device_id=(toward(way), col), device_id_type=MESH,
+        ).start()
     for u in range(1, direct):
         mixed(u)
-        told[u] = tell(u)
+        tell(u)
     for u in range(direct, early):
         mixed(u)
-
-    parts = []
     for d in range(1, n):
-        copy = pltpu.make_async_remote_copy(
+        pltpu.make_async_remote_copy(
             src_ref=mine.at[(me + d) % n], dst_ref=partial.at[d],
-            send_sem=part_send.at[d], recv_sem=part_recv.at[d], device_id=peer(d), device_id_type=MESH,
-        )
-        copy.start()
-        parts.append(copy)
-
-    for copy in smalls[1:]:
-        copy.wait()
+            send_sem=part_sem.at[0], recv_sem=part_sem.at[1], device_id=peer(d), device_id_type=MESH,
+        ).start()
+    wait_for(norm_held, small_sem.at[1])
+
     begin(0, heard_of(0))
 
-    for copy in parts:
-        copy.wait_recv()
+    wait_for(partial.at[pl.ds(1, n - 1)], part_sem.at[1])
     top = mine[me]
     for d in range(1, n):
         top = jnp.maximum(top, partial[d])
     whole[me, :, 0:block] = top
-    whole[me, :, block:block + piece] = train_held[...] + step_held[...]
-    wholes = []
+    whole[me, :, block:block + piece] = norm_held[0] + norm_held[1]
     for d in range(1, n):
-        copy = pltpu.make_async_remote_copy(
+        pltpu.make_async_remote_copy(
             src_ref=whole.at[me], dst_ref=whole.at[me],
-            send_sem=whole_send.at[d], recv_sem=whole_recv.at[d], device_id=peer(d), device_id_type=MESH,
-        )
-        copy.start()
-        wholes.append(copy)
+            send_sem=whole_sem.at[0], recv_sem=whole_sem.at[1], device_id=peer(d), device_id_type=MESH,
+        ).start()
 
     for u in range(1, direct):
         begin(u, heard_of(u))
 
-    for d in range(1, n):
-        pltpu.make_async_remote_copy(
-            src_ref=whole.at[me], dst_ref=whole.at[(me + (n - d)) % n],
-            send_sem=whole_send.at[d], recv_sem=whole_recv.at[d], device_id=peer(d), device_id_type=MESH,
-        ).wait_recv()
+    wait_for(whole.at[pl.ds(1, n - 1)], whole_sem.at[1])
     for b in range(n):
         w, first = b * block // cols, b * block % cols
         columns[w][:, first:first + block] = whole[b, :, 0:block]
@@ -365,28 +330,20 @@
         w, first, width = units[u]
         begin(u, 1.0 / columns[w][:, first:first + width])
 
-    w, first, width = units[early]
-    inverse = 1.0 / columns[w][:, first:first + width]
+    inverse = 1.0 / columns[e_weight][:, e_first:e_first + e_width]
+    wait_for(raw, raw_sem.at[1])
     for way in range(2):
-        aheads[way].wait_recv()
         scaled(early, origin_of(way, 1), inverse, lambda lines: raw[way, lines, :])
-        sent[way, 1, early] = ring(way, 1, early)
-        sent[way, 1, early].start()
     scaled(early, me, inverse, held(early))
 
-    norms = []
     for d in range(n):
         gains[0, d:d + 1, :] = whole[d, :, block:block + LANES]
     for d in range(1, k):
-        copy = pltpu.make_async_remote_copy(
-            src_ref=gains.at[0], dst_ref=gains.at[d],
-            send_sem=norm_send.at[d], recv_sem=norm_recv.at[d],
+        pltpu.make_async_remote_copy(
+            src_ref=gains.at[0], dst_ref=gains.at[d], send_sem=norm_sem.at[0], recv_sem=norm_sem.at[1],
             device_id=(me, (col + d) % k), device_id_type=MESH,
-        )
-        copy.start()
-        norms.append(copy)
-    for copy in norms:
-        copy.wait_recv()
+        ).start()
+    wait_for(gains.at[pl.ds(1, k - 1)], norm_sem.at[1])
     gain = jnp.concatenate([gains[(col + (k - j)) % k][:, 0:piece] for j in range(k)], axis=1)
     if serve_norm.shape[1] == gain.shape[1]:
         serve_norm[...] = gain.astype(jnp.bfloat16)
@@ -397,35 +354,53 @@
             gain_rows[i:i + 1, :] = gain[i // each:i // each + 1, at_lane:at_lane + LANES]
         serve_norm[...] = gain_rows[...].astype(jnp.bfloat16)
 
-    for hop in range(1, n // 2 + 1):
-        for u in range(len(units)):
+    last = n // 2 - 1
+    halves = ((0, cols // 2, ring_recv.at[last - 1, 1, 1]), (cols // 2, cols // 2, ring_recv.at[last, 0, 1]))
+
+    for hop in range(1, last + 1):
+        for w in range(2):
             for way in range(2):
-                if (way, hop - 1, u) not in sent:
-                    continue
-                sent[way, hop - 1, u].wait_recv()
-                if hop < n // 2 - 1 or (hop == n // 2 - 1 and way == units[u][0]):
-                    sent[way, hop, u] = ring(way, hop, u)
-                    sent[way, hop, u].start()
-
-    for copy in list(sent.values()) + aheads:
-        copy.wait_send()
-    for copy in sum(told.values(), norms + parts + wholes):
-        copy.wait_send()
+                split = (way, w) == (1, 1)
+                width = e_first if (hop, w) == (1, e_weight) else cols
+                if hop == last and split:
+                    for first, half, sem in halves:
+                        wait_for(place(origin_of(way, hop), w, first, half), sem)
+                        send(way, hop, w, first, half, ring_send.at[2, 0], ring_recv.at[hop, way, w])
+                elif hop < last or way == w:
+                    wait_for(place(origin_of(way, hop), w, 0, width), ring_recv.at[hop - 1, way, w])
+                    wait_for(place(me, w, 0, width), ring_send.at[way, w])
+                    if hop == last - 1 and split:
+                        for first, half, sem in halves:
+                            send(way, hop, w, first, half, ring_send.at[way, w], sem)
+                    else:
+                        send(way, hop, w, 0, cols, ring_send.at[way, w], ring_recv.at[hop, way, w])
+
+    for way in range(2):
+        wait_for(place(origin_of(way, last), 1 - way, 0, cols), ring_recv.at[last - 1, way, 1 - way])
+    for way in range(2):
+        wait_for(place(origin_of(way, last + 1), way, 0, cols), ring_recv.at[last, way, way])
+    for way in range(2):
+        for w in range(2):
+            wait_for(place(me, w, 0, cols), ring_send.at[way, w])
+    wait_for(place(me, 1, 0, cols), ring_send.at[2, 0])
+    wait_for(raw, raw_sem.at[0])
+    wait_for(heard.at[:, pl.ds(1, n - 1)], max_send.at[0])
+    wait_for(partial.at[pl.ds(1, n - 1)], part_sem.at[0])
+    wait_for(whole.at[pl.ds(1, n - 1)], whole_sem.at[0])
+    wait_for(gains.at[pl.ds(1, k - 1)], norm_sem.at[0])
 
 
 def writer(*refs):
     (sem,), count = refs[-1:], (len(refs) - 1) // 2
-    copies = []
-    for source, target in zip(refs[:count], refs[count:-1]):
+    pairs = list(zip(refs[:count], refs[count:-1]))
+    for i, (source, target) in enumerate(pairs):
         pieces = 4 if source.shape[0] > LANES else 1
         lines = source.shape[0] // pieces
         for p in range(pieces):
             span = pl.ds(p * lines, lines)
-            copies.append(pltpu.make_async_copy(source.at[span], target.at[span], sem.at[len(copies)]))
-    for copy in copies:
-        copy.start()
-    for copy in copies:
-        copy.wait()
+            pltpu.make_async_copy(source.at[span], target.at[span], sem.at[i]).start()
+    for i, (source, target) in enumerate(pairs):
+        pltpu.make_async_copy(source, target, sem.at[i]).wait()
 
 
 def solution(mesh):
@@ -435,7 +410,7 @@
         rows, cols = one_gate.shape
         piece = norm_train.shape[0]
         parts = 2 if n <= 8 else 1
-        near = n <= 8
+        near = 4 < n <= 8
         shaped = pltpu.VMEM if near else jax.ShapeDtypeStruct
         norm_shape = (n * k * piece // LANES, LANES) if k * piece % LANES == 0 else (n, k * piece)
         shapes = [
@@ -458,8 +433,10 @@
         if near:
             body = functools.partial(near_kernel, n, k, units, direct, early)
             small_spec = hbm
-            scratch = [pltpu.VMEM((2, rows, cols), jnp.float32)] * 3 + [
-                pltpu.VMEM((1, rows), jnp.float32), pltpu.VMEM((1, piece), jnp.float32), pltpu.VMEM((1, piece), jnp.float32),
+            scratch = [
+                pltpu.VMEM((2, 2, rows, cols), jnp.float32),
+                pltpu.VMEM((2, rows, cols), jnp.float32),
+                pltpu.VMEM((1, rows), jnp.float32), pltpu.VMEM((2, 1, piece), jnp.float32),
                 pltpu.VMEM((rows, LANES), jnp.float32),
                 pltpu.VMEM((2, rows, e), jnp.float32),
                 pltpu.VMEM((n, 1, block), jnp.float32),
@@ -467,10 +444,8 @@
                 pltpu.VMEM((n, 1, block), jnp.float32),
                 pltpu.VMEM((n, 1, block + LANES), jnp.float32),
             ] + gain_shapes + [
-                sems((len(units), 2)), sems((3,)), sems((2,)), sems((2,)),
-                sems((direct, n)), sems((direct, n)), sems((n,)), sems((n,)), sems((n,)), sems((n,)),
-                sems((k,)), sems((k,)),
-                sems((2, n // 2, len(units))), sems((2, n // 2, len(units))),
+                sems((len(units),)), sems((2,)), sems((2,)), sems((1,)), sems((direct,)), sems((2,)), sems((2,)), sems((2,)),
+                sems((3, 2)), sems((n // 2, 2, 2)),
             ]
         else:
             body = functools.partial(kernel, n, k, parts)
@@ -501,7 +476,7 @@
                 out_shape=[jax.ShapeDtypeStruct(*shape) for shape in shapes],
                 in_specs=[vmem] * 5,
                 out_specs=[hbm] * 5,
-                scratch_shapes=[pltpu.SemaphoreType.DMA((11,))],
+                scratch_shapes=[pltpu.SemaphoreType.DMA((5,))],
                 compiler_params=pltpu.CompilerParams(vmem_limit_bytes=2**20),
             )(*results)
         final_gate, final_up, column_gate, column_up, serve_norm = results

time: 175 us -> 174 us (level)
  Pallas kernels: 175 us -> 173 us
where the time goes in v3:
time: 174 us
  Pallas kernels  173 us (99%)
    pallas_call x1, Pallas kernels, local(): pl.pallas_call(body, out_shape=[shaped(*shape) for shape in shapes], in_s...  167 us
    pallas_call x1, Pallas kernels, local(): pl.pallas_call(writer, out_shape=[jax.ShapeDtypeStruct(*shape) for shape...  5.9 us

profile of v3, /device:TPU:0, one launch (start us, length us, event | category | flops | bytes accessed | tf_op | source)
XLA Modules:
  0.0 173.8 jit_solution(606227007580495908)
XLA Ops:
  0.6 167.3 %shard_map.110 = (bf16[2048,2048]{1,0:T(8,128)(2,1)S(1)}, bf16[2048,2048]{1,0:T(8,128)(2,1)S(1)}, f32[1,2048]{1,0:T(1,128)S(1)}, f32[1,2048]{1,0:T(1,128)S(1)}, bf16[16,128]{1,0:T(8,128)(2,1)S(1)}) custom-call(f32[256,2048]{1,0:T(8,128)} %one_gate.1, f32[256,2048]{1,0:T(8,128)} %other_gate.1, f32[256,2048]{1,0:T(8,128)} %one_up.1, f32[256,2048]{1,0:T(8,128)} %other_up.1, ...), custom_call_target="tpu_custom_call" | custom-call | tf_op jit(solution)/shard_map/pallas_call | solution.py:460
  167.9 5.9 %shard_map.111 = (bf16[2048,2048]{1,0:T(8,128)(2,1)}, bf16[2048,2048]{1,0:T(8,128)(2,1)}, f32[1,2048]{1,0:T(1,128)}, f32[1,2048]{1,0:T(1,128)}, bf16[16,128]{1,0:T(8,128)(2,1)}) custom-call(bf16[2048,2048]{1,0:T(8,128)(2,1)S(1)} %get-tuple-element.15.refs_0_, bf16[2048,2048]{1,0:T(8,128)(2,1)S(1)} %get-tuple-element.16.refs_1_, ...), custom_call_target="tpu_custom_call" | custom-call | tf_op jit(solution)/shard_map/pallas_call | solution.py:474

commit v4 on v3

--- a/solution.py
+++ b/solution.py
@@ -164,10 +164,87 @@
         copy.wait_send()
 
 
+class Ring:
+    def __init__(self, n, rows, blocks, sends, recvs):
+        self.n, self.rows, self.blocks, self.sends, self.recvs = n, rows, blocks, sends, recvs
+        self.me, self.col = lax.axis_index("shard"), lax.axis_index("model")
+        self.at = position_of(self.me, n)
+
+    def toward(self, way):
+        return index_at((self.at + (1 if way == 0 else self.n - 1)) % self.n, self.n)
+
+    def origin_of(self, way, hop):
+        return index_at((self.at + (self.n - hop if way == 0 else hop)) % self.n, self.n)
+
+    def place(self, b, origin, first, width):
+        ref, start = self.blocks[b][0:2]
+        lines = pl.ds(pl.multiple_of(origin * self.rows, self.rows), self.rows)
+        return ref.at[lines, pl.ds(start + first, width)]
+
+    def send(self, way, hop, b, first, width, source=None):
+        part = self.place(b, self.origin_of(way, hop), first, width)
+        pltpu.make_async_remote_copy(
+            src_ref=part if source is None else source, dst_ref=part,
+            send_sem=self.sends.at[way, b], recv_sem=self.recvs.at[hop, way, b],
+            device_id=(self.toward(way), self.col), device_id_type=MESH,
+        ).start()
+
+    def arrived(self, way, hop, b, first, width):
+        wait_for(self.place(b, self.origin_of(way, hop + 1), first, width), self.recvs.at[hop, way, b])
+
+    def final_part(self, way, b):
+        width = self.blocks[b][2]
+        if b < 2:
+            return (0, width) if way == b else None
+        return (way * (width // 2), width // 2)
+
+    def each(self, act):
+        for i in range(len(self.blocks)):
+            for way in range(2):
+                b = (i, 1 - i if i < 2 else i)[way]
+                only = self.blocks[b][4]
+                if only is None:
+                    act(way, b)
+                else:
+                    pl.when(only)(functools.partial(act, way, b))
+
+    def go(self):
+        last = self.n // 2 - 1
+        for hop in range(1, last + 1):
+            def forward(way, b, hop=hop):
+                width = self.blocks[b][3 if hop == 1 else 2]
+                part = (0, self.blocks[b][2]) if hop < last else self.final_part(way, b)
+                if part is not None:
+                    self.arrived(way, hop - 1, b, 0, width)
+                    wait_for(self.place(b, self.me, 0, width), self.sends.at[way, b])
+                    self.send(way, hop, b, *part)
+            self.each(forward)
+
+        def rest(way, b):
+            if self.final_part(way, b) is None:
+                self.arrived(way, last - 1, b, 0, self.blocks[b][2])
+
+        def end(way, b):
+            part = self.final_part(way, b)
+            if part is not None:
+                self.arrived(way, last, b, *part)
+
+        def drain(way, b):
+            part = self.final_part(way, b) or (0, self.blocks[b][2])
+            wait_for(self.place(b, self.me, *part), self.sends.at[way, b])
+
+        for act in (rest, end, drain):
+            self.each(act)
+
+
+def wait_for(ref, sem):
+    pltpu.make_async_copy(ref, ref, sem).wait()
+
+
 def near_kernel(
     n, k, units, direct, early,
     one_gate, other_gate, one_up, other_up, mix, norm_train, norm_step,
-    final_gate, final_up, column_gate, column_up, serve_norm,
+    final_gate, column_gate, column_up, serve_norm, own_up, extra,
     taken, result, mix_held, norm_held, share, raw, mine, heard, partial, whole, gains, gain_rows,
     load_sem, small_sem, raw_sem, max_send, max_recv, part_sem, whole_sem, norm_sem, ring_send, ring_recv,
 ):
@@ -175,16 +252,13 @@
     piece = norm_train.shape[1]
     block = mine.shape[2]
     me, col = lax.axis_index("shard"), lax.axis_index("model")
-    at = position_of(me, n)
 
     ones, others = (one_gate, one_up), (other_gate, other_up)
-    finals, columns = (final_gate, final_up), (column_gate, column_up)
+    columns = (column_gate, column_up)
+    odd = col % 2 == 1
 
     def peer(d):
         return ((me + d) % n, col)
-
-    def wait_for(ref, sem):
-        pltpu.make_async_copy(ref, ref, sem).wait()
 
     def load(u):
         w, first, width = units[u]
@@ -245,43 +319,36 @@
             top = jnp.maximum(top, heard[u, d])
         return 1.0 / top
 
-    def toward(way):
-        return index_at((at + (1 if way == 0 else n - 1)) % n, n)
-
-    def origin_of(way, hop):
-        return index_at((at + (n - hop if way == 0 else hop)) % n, n)
-
-    def place(origin, w, first, width):
-        return finals[w].at[pl.ds(pl.multiple_of(origin * rows, rows), rows), pl.ds(first, width)]
-
-    def send(way, hop, w, first, width, send_sem, recv_sem):
-        part = place(origin_of(way, hop), w, first, width)
-        pltpu.make_async_remote_copy(
-            src_ref=part, dst_ref=part, send_sem=send_sem, recv_sem=recv_sem,
-            device_id=(toward(way), col), device_id_type=MESH,
-        ).start()
-
     e_weight, e_first, e_width = units[early]
-
-    def scaled(u, origin, inverse, read):
-        w, first, width = units[u]
-
+    half = cols // 2
+    shared = extra.shape[1]
+    ring = Ring(
+        n, rows,
+        (
+            (final_gate, 0, half, half, None), (final_gate, half, half, half - e_width, None),
+            (extra, 0, shared, shared, odd),
+        ),
+        ring_send, ring_recv,
+    )
+
+    def scaled(target, origin, first, width, inverse, read):
         def step(g, _):
             start = pl.multiple_of(g * 16, 16)
             to = pl.multiple_of(origin * rows + g * 16, 16)
-            finals[w][pl.ds(to, 16), pl.ds(first, width)] = (read(pl.ds(start, 16)) * inverse).astype(jnp.bfloat16)
+            target[pl.ds(to, 16), pl.ds(first, width)] = (read(pl.ds(start, 16)) * inverse).astype(jnp.bfloat16)
             return 0
 
         lax.fori_loop(0, rows // 16, step, 0, unroll=2)
 
-    def held(u):
+    def held(w, first, width):
+        return lambda lines: result[w, lines, pl.ds(first, width)]
+
+    def begin(u, inverse):
         w, first, width = units[u]
-        return lambda lines: result[w, lines, pl.ds(first, width)]
-
-    def begin(u, inverse):
-        scaled(u, me, inverse, held(u))
+        scaled(final_gate, me, first, width, inverse, held(w, first, width))
         for way in range(2):
-            send(way, 0, *units[u], ring_send.at[way, units[u][0]], ring_recv.at[0, way, units[u][0]])
+            b = first // half
+            ring.send(way, 0, b, first - b * half, width)
 
     mixed(0)
     pl.semaphore_wait(barrier, n - 1 + k - 1)
@@ -290,7 +357,7 @@
     for way in range(2):
         pltpu.make_async_remote_copy(
             src_ref=result.at[e_weight, :, pl.ds(e_first, e_width)], dst_ref=raw.at[way],
-            send_sem=raw_sem.at[0], recv_sem=raw_sem.at[1], device_id=(toward(way), col), device_id_type=MESH,
+            send_sem=raw_sem.at[0], recv_sem=raw_sem.at[1], device_id=(ring.toward(way), col), device_id_type=MESH,
         ).start()
     for u in range(1, direct):
         mixed(u)
@@ -328,13 +395,23 @@
 
     for u in range(direct, early):
         w, first, width = units[u]
-        begin(u, 1.0 / columns[w][:, first:first + width])
+        if w == 0:
+            begin(u, 1.0 / columns[0][:, first:first + width])
+
+    inverse_up = 1.0 / columns[1][...]
+    scaled(own_up, 0, 0, cols, inverse_up, held(1, 0, cols))
+
+    @pl.when(odd)
+    def _():
+        scaled(extra, me, 0, shared, inverse_up[:, 0:shared], held(1, 0, shared))
+        for way in range(2):
+            ring.send(way, 0, 2, 0, shared, own_up.at[:, pl.ds(0, shared)])
 
     inverse = 1.0 / columns[e_weight][:, e_first:e_first + e_width]
     wait_for(raw, raw_sem.at[1])
     for way in range(2):
-        scaled(early, origin_of(way, 1), inverse, lambda lines: raw[way, lines, :])
-    scaled(early, me, inverse, held(early))
+        scaled(final_gate, ring.origin_of(way, 1), e_first, e_width, inverse, lambda lines: raw[way, lines, :])
+    scaled(final_gate, me, e_first, e_width, inverse, held(e_weight, e_first, e_width))
 
     for d in range(n):
         gains[0, d:d + 1, :] = whole[d, :, block:block + LANES]
@@ -354,35 +431,7 @@
             gain_rows[i:i + 1, :] = gain[i // each:i // each + 1, at_lane:at_lane + LANES]
         serve_norm[...] = gain_rows[...].astype(jnp.bfloat16)
 
-    last = n // 2 - 1
-    halves = ((0, cols // 2, ring_recv.at[last - 1, 1, 1]), (cols // 2, cols // 2, ring_recv.at[last, 0, 1]))
-
-    for hop in range(1, last + 1):
-        for w in range(2):
-            for way in range(2):
-                split = (way, w) == (1, 1)
-                width = e_first if (hop, w) == (1, e_weight) else cols
-                if hop == last and split:
-                    for first, half, sem in halves:
-                        wait_for(place(origin_of(way, hop), w, first, half), sem)
-                        send(way, hop, w, first, half, ring_send.at[2, 0], ring_recv.at[hop, way, w])
-                elif hop < last or way == w:
-                    wait_for(place(origin_of(way, hop), w, 0, width), ring_recv.at[hop - 1, way, w])
-                    wait_for(place(me, w, 0, width), ring_send.at[way, w])
-                    if hop == last - 1 and split:
-                        for first, half, sem in halves:
-                            send(way, hop, w, first, half, ring_send.at[way, w], sem)
-                    else:
-                        send(way, hop, w, 0, cols, ring_send.at[way, w], ring_recv.at[hop, way, w])
-
-    for way in range(2):
-        wait_for(place(origin_of(way, last), 1 - way, 0, cols), ring_recv.at[last - 1, way, 1 - way])
-    for way in range(2):
-        wait_for(place(origin_of(way, last + 1), way, 0, cols), ring_recv.at[last, way, way])
-    for way in range(2):
-        for w in range(2):
-            wait_for(place(me, w, 0, cols), ring_send.at[way, w])
-    wait_for(place(me, 1, 0, cols), ring_send.at[2, 0])
+    ring.go()
     wait_for(raw, raw_sem.at[0])
     wait_for(heard.at[:, pl.ds(1, n - 1)], max_send.at[0])
     wait_for(partial.at[pl.ds(1, n - 1)], part_sem.at[0])
@@ -390,15 +439,62 @@
     wait_for(gains.at[pl.ds(1, k - 1)], norm_sem.at[0])
 
 
-def writer(*refs):
-    (sem,), count = refs[-1:], (len(refs) - 1) // 2
-    pairs = list(zip(refs[:count], refs[count:-1]))
+def second_kernel(n, own_up, extra, after, final_up, ring_send, ring_recv):
+    rows, cols = own_up.shape
+    shared = extra.shape[1]
+    half = (cols - shared) // 2
+    even = lax.axis_index("model") % 2 == 0
+    ring = Ring(
+        n, rows,
+        (
+            (final_up, shared, half, half, None), (final_up, shared + half, half, half, None),
+            (final_up, 0, shared, shared, even),
+        ),
+        ring_send, ring_recv,
+    )
+    barrier = pltpu.get_barrier_semaphore()
+    for way in range(2):
+        pl.semaphore_signal(barrier, inc=1, device_id=(ring.toward(way), ring.col), device_id_type=MESH)
+    pl.semaphore_wait(barrier, 2)
+
+    def first_hop(way, b):
+        _, start, width, _, _ = ring.blocks[b]
+        ring.send(way, 0, b, 0, width, own_up.at[:, pl.ds(start, width)])
+
+    ring.each(first_hop)
+
+    def copied(source, to, first, width, lines):
+        def step(g, _):
+            start = pl.multiple_of(g * 16, 16)
+            final_up[pl.ds(pl.multiple_of(to + start, 16), 16), pl.ds(first, width)] = source[pl.ds(start, 16), pl.ds(first, width)]
+            return 0
+
+        lax.fori_loop(0, lines // 16, step, 0, unroll=2)
+
+    copied(own_up, ring.me * rows, shared, cols - shared, rows)
+
+    @pl.when(even)
+    def _():
+        copied(own_up, ring.me * rows, 0, shared, rows)
+
+    @pl.when(jnp.logical_not(even))
+    def _():
+        copied(extra, 0, 0, shared, n * rows)
+
+    ring.go()
+
+
+def writer(count, *refs):
+    sem = refs[-1]
+    pairs = list(zip(refs[:count], refs[count:2 * count]))
     for i, (source, target) in enumerate(pairs):
         pieces = 4 if source.shape[0] > LANES else 1
         lines = source.shape[0] // pieces
         for p in range(pieces):
             span = pl.ds(p * lines, lines)
             pltpu.make_async_copy(source.at[span], target.at[span], sem.at[i]).start()
+    for after in refs[2 * count:-1]:
+        after[...] = jnp.zeros_like(after)
     for i, (source, target) in enumerate(pairs):
         pltpu.make_async_copy(source, target, sem.at[i]).wait()
 
@@ -411,75 +507,90 @@
         piece = norm_train.shape[0]
         parts = 2 if n <= 8 else 1
         near = 4 < n <= 8
-        shaped = pltpu.VMEM if near else jax.ShapeDtypeStruct
         norm_shape = (n * k * piece // LANES, LANES) if k * piece % LANES == 0 else (n, k * piece)
         shapes = [
             ((n * rows, cols), jnp.bfloat16), ((n * rows, cols), jnp.bfloat16),
             ((1, cols), jnp.float32), ((1, cols), jnp.float32), (norm_shape, jnp.bfloat16),
         ]
         hbm, vmem = pl.BlockSpec(memory_space=pltpu.HBM), pl.BlockSpec(memory_space=pltpu.VMEM)
-        block = 2 * cols // n
-        e = cols // 16
-        units = (
-            (0, 0, block), (0, block, block), (0, 2 * block, cols - 2 * block),
-            (1, 0, 8 * e), (1, 8 * e, 7 * e), (1, 15 * e, e),
-        )
-        direct, early = 2, len(units) - 1
+        sems = pltpu.SemaphoreType.DMA
         gain_shapes = [
             pltpu.VMEM((k, n, LANES), jnp.float32),
             pltpu.VMEM((max(n * k * piece // LANES, 8), LANES), jnp.float32),
         ]
-        sems = pltpu.SemaphoreType.DMA
-        if near:
-            body = functools.partial(near_kernel, n, k, units, direct, early)
-            small_spec = hbm
-            scratch = [
-                pltpu.VMEM((2, 2, rows, cols), jnp.float32),
-                pltpu.VMEM((2, rows, cols), jnp.float32),
-                pltpu.VMEM((1, rows), jnp.float32), pltpu.VMEM((2, 1, piece), jnp.float32),
-                pltpu.VMEM((rows, LANES), jnp.float32),
-                pltpu.VMEM((2, rows, e), jnp.float32),
-                pltpu.VMEM((n, 1, block), jnp.float32),
-                pltpu.VMEM((direct, n, 1, block), jnp.float32),
-                pltpu.VMEM((n, 1, block), jnp.float32),
-                pltpu.VMEM((n, 1, block + LANES), jnp.float32),
-            ] + gain_shapes + [
-                sems((len(units),)), sems((2,)), sems((2,)), sems((1,)), sems((direct,)), sems((2,)), sems((2,)), sems((2,)),
-                sems((3, 2)), sems((n // 2, 2, 2)),
-            ]
-        else:
-            body = functools.partial(kernel, n, k, parts)
-            small_spec = vmem
-            scratch = [pltpu.VMEM((2, rows, cols), jnp.float32)] * 2 + [
-                pltpu.VMEM((rows, LANES), jnp.float32),
-                pltpu.VMEM((2, parts, n, 1, cols // parts + LANES), jnp.float32),
-            ] + gain_shapes + [
-                sems((2, parts, 2)), sems((2, parts, n)), sems((2, parts, n)), sems((k,)), sems((k,)),
-                sems((2, n // 2, 2, parts)), sems((2, n // 2, 2, parts)),
-            ]
-        results = pl.pallas_call(
-            body,
-            out_shape=[shaped(*shape) for shape in shapes],
-            in_specs=[hbm] * 4 + [small_spec] * 3,
-            out_specs=[vmem] * 5,
-            scratch_shapes=scratch,
-            compiler_params=pltpu.CompilerParams(
-                collective_id=0, has_side_effects=True, vmem_limit_bytes=46 * 2**20
-            ),
-        )(
+        operands = (
             one_gate, other_gate, one_up, other_up,
             mix_share.reshape(1, rows), norm_train.reshape(1, piece), norm_step.reshape(1, piece),
         )
+
+        def written(arrays, order):
+            count = len(arrays)
+            return pl.pallas_call(
+                functools.partial(writer, count),
+                out_shape=[jax.ShapeDtypeStruct(x.shape, x.dtype) for x in arrays] + [pltpu.VMEM((8, LANES), jnp.float32)] * order,
+                in_specs=[vmem] * count,
+                out_specs=[hbm] * count + [vmem] * order,
+                scratch_shapes=[sems((count,))],
+                compiler_params=pltpu.CompilerParams(vmem_limit_bytes=2**20),
+            )(*arrays)
+
         if near:
-            results = pl.pallas_call(
-                writer,
+            block = 2 * cols // n
+            e = cols // 16
+            shared = cols * 3 // 8
+            units = (
+                (0, 0, block), (0, block, block), (0, 8 * e, 7 * e),
+                (1, 0, 8 * e), (1, 8 * e, 8 * e), (0, 15 * e, e),
+            )
+            direct, early = 2, len(units) - 1
+            final_gate, column_gate, column_up, serve_norm, own_up, extra = pl.pallas_call(
+                functools.partial(near_kernel, n, k, units, direct, early),
+                out_shape=[pltpu.VMEM(*shape) for shape in shapes[0:1] + shapes[2:5]] + [
+                    pltpu.VMEM((rows, cols), jnp.bfloat16), pltpu.VMEM((n * rows, shared), jnp.bfloat16),
+                ],
+                in_specs=[hbm] * 7,
+                out_specs=[vmem] * 6,
+                scratch_shapes=[
+                    pltpu.VMEM((2, 2, rows, cols), jnp.float32),
+                    pltpu.VMEM((2, rows, cols), jnp.float32),
+                    pltpu.VMEM((1, rows), jnp.float32), pltpu.VMEM((2, 1, piece), jnp.float32),
+                    pltpu.VMEM((rows, LANES), jnp.float32),
+                    pltpu.VMEM((2, rows, e), jnp.float32),
+                    pltpu.VMEM((n, 1, block), jnp.float32),
+                    pltpu.VMEM((direct, n, 1, block), jnp.float32),
+                    pltpu.VMEM((n, 1, block), jnp.float32),
+                    pltpu.VMEM((n, 1, block + LANES), jnp.float32),
+                ] + gain_shapes + [
+                    sems((len(units),)), sems((2,)), sems((2,)), sems((1,)), sems((direct,)), sems((2,)), sems((2,)), sems((2,)),
+                    sems((2, 3)), sems((n // 2, 2, 3)),
+                ],
+                compiler_params=pltpu.CompilerParams(collective_id=0, has_side_effects=True, vmem_limit_bytes=51 * 2**20),
+            )(*operands)
+            final_gate, column_gate, column_up, serve_norm, after = written((final_gate, column_gate, column_up, serve_norm), 1)
+            final_up = pl.pallas_call(
+                functools.partial(second_kernel, n),
+                out_shape=pltpu.VMEM(*shapes[1]),
+                in_specs=[vmem] * 3,
+                out_specs=vmem,
+                scratch_shapes=[sems((2, 3)), sems((n // 2, 2, 3))],
+                compiler_params=pltpu.CompilerParams(collective_id=1, has_side_effects=True, vmem_limit_bytes=2**20),
+            )(own_up, extra, after)
+            (final_up,) = written((final_up,), 0)
+        else:
+            final_gate, final_up, column_gate, column_up, serve_norm = pl.pallas_call(
+                functools.partial(kernel, n, k, parts),
                 out_shape=[jax.ShapeDtypeStruct(*shape) for shape in shapes],
-                in_specs=[vmem] * 5,
-                out_specs=[hbm] * 5,
-                scratch_shapes=[pltpu.SemaphoreType.DMA((5,))],
-                compiler_params=pltpu.CompilerParams(vmem_limit_bytes=2**20),
-            )(*results)
-        final_gate, final_up, column_gate, column_up, serve_norm = results
+                in_specs=[hbm] * 4 + [vmem] * 3,
+                out_specs=[vmem] * 5,
+                scratch_shapes=[pltpu.VMEM((2, rows, cols), jnp.float32)] * 2 + [
+                    pltpu.VMEM((rows, LANES), jnp.float32),
+                    pltpu.VMEM((2, parts, n, 1, cols // parts + LANES), jnp.float32),
+                ] + gain_shapes + [
+                    sems((2, parts, 2)), sems((2, parts, n)), sems((2, parts, n)), sems((k,)), sems((k,)),
+                    sems((2, n // 2, 2, parts)), sems((2, n // 2, 2, parts)),
+                ],
+                compiler_params=pltpu.CompilerParams(collective_id=0, has_side_effects=True, vmem_limit_bytes=46 * 2**20),
+            )(*operands)
         return (
             final_gate, final_up, column_gate.reshape(cols), column_up.reshape(cols),
             serve_norm.reshape(n * k * piece),

time: 174 us -> 171 us (0.983)
  Pallas kernels: 173 us -> 170 us
    pallas_call x2 -> x4, Pallas kernels: 173 us -> 170 us  [the longest x1 92.5 us: local(): pl.pallas_call(functools.partial(near_kernel, n, k, units, direct, early)...]
where the time goes in v4:
time: 171 us
  Pallas kernels  170 us (99%)
    pallas_call x1, Pallas kernels, local(): pl.pallas_call(functools.partial(near_kernel, n, k, units, direct, early)...  92.5 us
    pallas_call x1, Pallas kernels, local(): pl.pallas_call(functools.partial(second_kernel, n), out_shape=pltpu.VMEM(...  71.3 us
    pallas_call x2, Pallas kernels, written(): pl.pallas_call(functools.partial(writer, count), out_shape=[jax.ShapeDtyp...  6.71 us

profile of v4, /device:TPU:0, one launch (start us, length us, event | category | flops | bytes accessed | tf_op | source)
XLA Modules:
  0.0 171.1 jit_solution(12480982957009955100)
XLA Ops:
  0.6 92.5 %shard_map.110 = (bf16[2048,2048]{1,0:T(8,128)(2,1)S(1)}, f32[1,2048]{1,0:T(1,128)S(1)}, f32[1,2048]{1,0:T(1,128)S(1)}, bf16[16,128]{1,0:T(8,128)(2,1)S(1)}, bf1...) custom-call(f32[256,2048]{1,0:T(8,128)} %one_gate.1, f32[256,2048]{1,0:T(8,128)} %other_gate.1, ...), custom_call_target="tpu_custom_call" | custom-call | tf_op jit(solution)/shard_map/pallas_call | solution.py:546
  93.2 3.4 %shard_map.111 = (bf16[2048,2048]{1,0:T(8,128)(2,1)}, f32[1,2048]{1,0:T(1,128)}, f32[1,2048]{1,0:T(1,128)}, bf16[16,128]{1,0:T(8,128)(2,1)}, f32[8,128]{1,0:T(8,128)S(1)}) custom-call(bf16[2048,2048]{1,0:T(8,128)(2,1)S(1)} %get-tuple-element.16.refs_0_, f32[1,2048]{1,0:T(1,128)S(1)} %get-tuple-element.17.refs_1_, f32[1,2048]{1,0:T(1,128)S(1)} %get-tuple-element.18.refs_2_, ...), custom_call_target="tpu_custom_call" | custom-call | tf_op jit(solution)/shard_map/pallas_call | solution.py:528
  96.5 71.3 %shard_map.112.refs_0_ = bf16[2048,2048]{1,0:T(8,128)(2,1)S(1)} custom-call(bf16[256,2048]{1,0:T(8,128)(2,1)S(1)} %get-tuple-element.21.own_up, bf16[2048,768]{1,0:T(8,128)(2,1)S(1)} %get-tuple-element.22.extra, f32[8,128]{1,0:T(8,128)S(1)} %get-tuple-element.23.after), custom_call_target="tpu_custom_call" | custom-call | tf_op jit(solution)/shard_map/pallas_call | solution.py:570
  167.8 3.3 %shard_map.113 = bf16[2048,2048]{1,0:T(8,128)(2,1)} custom-call(bf16[2048,2048]{1,0:T(8,128)(2,1)S(1)} %shard_map.112.refs_0_), custom_call_target="tpu_custom_call" | custom-call | tf_op jit(solution)/shard_map/pallas_call | solution.py:528

commit v5 on v4

--- a/solution.py
+++ b/solution.py
@@ -9,6 +9,9 @@
 
 MESH = pl.DeviceIdType.MESH
 LANES = 128
+SHARED = 5
+LEADER = 0
+PIECES = 8
 
 
 def position_of(index, n):
@@ -255,7 +258,7 @@
 
     ones, others = (one_gate, one_up), (other_gate, other_up)
     columns = (column_gate, column_up)
-    odd = col % 2 == 1
+    odd = leads(col)
 
     def peer(d):
         return ((me + d) % n, col)
@@ -439,11 +442,14 @@
     wait_for(gains.at[pl.ds(1, k - 1)], norm_sem.at[0])
 
 
-def second_kernel(n, own_up, extra, after, final_up, ring_send, ring_recv):
+def leads(col):
+    return col % 2 == LEADER
+
+
+def second_kernel(n, shared, own_up, after, final_up, ring_send, ring_recv):
     rows, cols = own_up.shape
-    shared = extra.shape[1]
     half = (cols - shared) // 2
-    even = lax.axis_index("model") % 2 == 0
+    even = jnp.logical_not(leads(lax.axis_index("model")))
     ring = Ring(
         n, rows,
         (
@@ -463,40 +469,47 @@
 
     ring.each(first_hop)
 
-    def copied(source, to, first, width, lines):
-        def step(g, _):
-            start = pl.multiple_of(g * 16, 16)
-            final_up[pl.ds(pl.multiple_of(to + start, 16), 16), pl.ds(first, width)] = source[pl.ds(start, 16), pl.ds(first, width)]
-            return 0
-
-        lax.fori_loop(0, lines // 16, step, 0, unroll=2)
-
-    copied(own_up, ring.me * rows, shared, cols - shared, rows)
-
-    @pl.when(even)
-    def _():
-        copied(own_up, ring.me * rows, 0, shared, rows)
-
-    @pl.when(jnp.logical_not(even))
-    def _():
-        copied(extra, 0, 0, shared, n * rows)
-
+    def step(g, _):
+        start = pl.multiple_of(g * 16, 16)
+        final_up[pl.ds(pl.multiple_of(ring.me * rows + start, 16), 16), :] = own_up[pl.ds(start, 16), :]
+        return 0
+
+    lax.fori_loop(0, rows // 16, step, 0, unroll=2)
     ring.go()
 
 
-def writer(count, *refs):
-    sem = refs[-1]
-    pairs = list(zip(refs[:count], refs[count:2 * count]))
-    for i, (source, target) in enumerate(pairs):
-        pieces = 4 if source.shape[0] > LANES else 1
-        lines = source.shape[0] // pieces
-        for p in range(pieces):
-            span = pl.ds(p * lines, lines)
-            pltpu.make_async_copy(source.at[span], target.at[span], sem.at[i]).start()
-    for after in refs[2 * count:-1]:
-        after[...] = jnp.zeros_like(after)
-    for i, (source, target) in enumerate(pairs):
+def out(source, target, sem):
+    pieces = PIECES if source.shape[0] > LANES else 1
+    lines = source.shape[0] // pieces
+    for p in range(pieces):
+        span = pl.ds(p * lines, lines)
+        pltpu.make_async_copy(source.at[span], target.at[span], sem).start()
+
+
+def first_writer(final_gate, column_gate, column_up, serve_norm, extra, gate_out, gate_column, up_column, norm_out, up_out, after, sem):
+    whole = ((final_gate, gate_out), (column_gate, gate_column), (column_up, up_column), (serve_norm, norm_out))
+    lead = leads(lax.axis_index("model"))
+    part = up_out.at[:, pl.ds(0, extra.shape[1])]
+    for i, (source, target) in enumerate(whole):
+        out(source, target, sem.at[i])
+    pl.when(lead)(lambda: out(extra, part, sem.at[len(whole)]))
+    after[...] = jnp.zeros_like(after)
+    for i, (source, target) in enumerate(whole):
         pltpu.make_async_copy(source, target, sem.at[i]).wait()
+    pl.when(lead)(lambda: pltpu.make_async_copy(extra, part, sem.at[len(whole)]).wait())
+
+
+def last_writer(shared, final_up, up_in, up_out, sem):
+    lead = leads(lax.axis_index("model"))
+    cols = final_up.shape[1]
+
+    def write(first):
+        span = pl.ds(first, cols - first)
+        out(final_up.at[:, span], up_out.at[:, span], sem.at[0])
+        pltpu.make_async_copy(final_up.at[:, span], up_out.at[:, span], sem.at[0]).wait()
+
+    pl.when(lead)(functools.partial(write, shared))
+    pl.when(jnp.logical_not(lead))(functools.partial(write, 0))
 
 
 def solution(mesh):
@@ -523,21 +536,10 @@
             mix_share.reshape(1, rows), norm_train.reshape(1, piece), norm_step.reshape(1, piece),
         )
 
-        def written(arrays, order):
-            count = len(arrays)
-            return pl.pallas_call(
-                functools.partial(writer, count),
-                out_shape=[jax.ShapeDtypeStruct(x.shape, x.dtype) for x in arrays] + [pltpu.VMEM((8, LANES), jnp.float32)] * order,
-                in_specs=[vmem] * count,
-                out_specs=[hbm] * count + [vmem] * order,
-                scratch_shapes=[sems((count,))],
-                compiler_params=pltpu.CompilerParams(vmem_limit_bytes=2**20),
-            )(*arrays)
-
         if near:
             block = 2 * cols // n
             e = cols // 16
-            shared = cols * 3 // 8
+            shared = cols // 8 * SHARED
             units = (
                 (0, 0, block), (0, block, block), (0, 8 * e, 7 * e),
                 (1, 0, 8 * e), (1, 8 * e, 8 * e), (0, 15 * e, e),
@@ -564,18 +566,34 @@
                     sems((len(units),)), sems((2,)), sems((2,)), sems((1,)), sems((direct,)), sems((2,)), sems((2,)), sems((2,)),
                     sems((2, 3)), sems((n // 2, 2, 3)),
                 ],
-                compiler_params=pltpu.CompilerParams(collective_id=0, has_side_effects=True, vmem_limit_bytes=51 * 2**20),
+                compiler_params=pltpu.CompilerParams(collective_id=0, has_side_effects=True, vmem_limit_bytes=(54 - SHARED) * 2**20),
             )(*operands)
-            final_gate, column_gate, column_up, serve_norm, after = written((final_gate, column_gate, column_up, serve_norm), 1)
-            final_up = pl.pallas_call(
-                functools.partial(second_kernel, n),
+            full = [jax.ShapeDtypeStruct(*shape) for shape in shapes]
+            final_gate, column_gate, column_up, serve_norm, final_up, after = pl.pallas_call(
+                first_writer,
+                out_shape=[full[0], full[2], full[3], full[4], full[1], pltpu.VMEM((8, LANES), jnp.float32)],
+                in_specs=[vmem] * 5,
+                out_specs=[hbm] * 5 + [vmem],
+                scratch_shapes=[sems((5,))],
+                compiler_params=pltpu.CompilerParams(vmem_limit_bytes=2**20),
+            )(final_gate, column_gate, column_up, serve_norm, extra)
+            gathered = pl.pallas_call(
+                functools.partial(second_kernel, n, shared),
                 out_shape=pltpu.VMEM(*shapes[1]),
-                in_specs=[vmem] * 3,
+                in_specs=[vmem] * 2,
                 out_specs=vmem,
                 scratch_shapes=[sems((2, 3)), sems((n // 2, 2, 3))],
                 compiler_params=pltpu.CompilerParams(collective_id=1, has_side_effects=True, vmem_limit_bytes=2**20),
-            )(own_up, extra, after)
-            (final_up,) = written((final_up,), 0)
+            )(own_up, after)
+            final_up = pl.pallas_call(
+                functools.partial(last_writer, shared),
+                out_shape=full[1],
+                in_specs=[vmem, hbm],
+                out_specs=hbm,
+                scratch_shapes=[sems((1,))],
+                input_output_aliases={1: 0},
+                compiler_params=pltpu.CompilerParams(vmem_limit_bytes=2**20),
+            )(gathered, final_up)
         else:
             final_gate, final_up, column_gate, column_up, serve_norm = pl.pallas_call(
                 functools.partial(kernel, n, k, parts),

time: 171 us -> 170 us (level)
    pallas_call x3, Pallas kernels: 78 us -> 38.1 us  [the longest x1 31.5 us: local(): pl.pallas_call(functools.partial(second_kernel, n, shared), out_shape=plt...]
    pallas_call x1, Pallas kernels: 92.5 us -> 131 us  [local(): pl.pallas_call(functools.partial(near_kernel, n, k, units, direct, early)...]
where the time goes in v5:
time: 170 us; the launch traced here: 169 us
  Pallas kernels  169 us (99%)
    pallas_call x1, Pallas kernels, local(): pl.pallas_call(functools.partial(near_kernel, n, k, units, direct, early)...  131 us
    pallas_call x1, Pallas kernels, local(): pl.pallas_call(functools.partial(second_kernel, n, shared), out_shape=plt...  31.5 us
    pallas_call x1, Pallas kernels, local(): pl.pallas_call(first_writer, out_shape=[full[0], full[2], full[3], full[4...  4.92 us

profile of v5, /device:TPU:0, one launch (start us, length us, event | category | flops | bytes accessed | tf_op | source)
XLA Modules:
  0.0 169.5 jit_solution(13954621702481590397)
XLA Ops:
  0.6 130.7 %shard_map.110 = (bf16[2048,2048]{1,0:T(8,128)(2,1)S(1)}, f32[1,2048]{1,0:T(1,128)S(1)}, f32[1,2048]{1,0:T(1,128)S(1)}, bf16[16,128]{1,0:T(8,128)(2,1)S(1)}, bf1...) custom-call(f32[256,2048]{1,0:T(8,128)} %one_gate.1, f32[256,2048]{1,0:T(8,128)} %other_gate.1, ...), custom_call_target="tpu_custom_call" | custom-call | tf_op jit(solution)/shard_map/pallas_call | solution.py:548
  131.4 4.9 %shard_map.111 = (bf16[2048,2048]{1,0:T(8,128)(2,1)}, f32[1,2048]{1,0:T(1,128)}, f32[1,2048]{1,0:T(1,128)}, bf16[16,128]{1,0:T(8,128)(2,1)}, bf16[2048,2048]{1,0:T(8,128)(2,1)}, /*index=5*/f32[8,128]{1,0:T(8,128)S(1)}) custom-call(bf16[2048,2048]{1,0:T(8,128)(2,1)S(1)} %get-tuple-element.17.final_gate, f32[1,2048]{1,0:T(1,128)S(1)} %get-tuple-element.18.column_gate, ...), custom_call_target="tpu_custom_call" | custom-call | tf_op jit(solution)/shard_map/pallas_call | solution.py:572
  136.3 31.5 %shard_map.112.final_up = bf16[2048,2048]{1,0:T(8,128)(2,1)S(1)} custom-call(bf16[256,2048]{1,0:T(8,128)(2,1)S(1)} %get-tuple-element.23.own_up, f32[8,128]{1,0:T(8,128)S(1)} %get-tuple-element.24.after), custom_call_target="tpu_custom_call" | custom-call | tf_op jit(solution)/shard_map/pallas_call | solution.py:580
  167.8 1.7 shard_map.113

commit v6 on v5

--- a/solution.py
+++ b/solution.py
@@ -9,7 +9,8 @@
 
 MESH = pl.DeviceIdType.MESH
 LANES = 128
-SHARED = 5
+SHARED = 3
+MORE = 2
 LEADER = 0
 PIECES = 8
 
@@ -245,7 +246,7 @@
 
 
 def near_kernel(
-    n, k, units, direct, early,
+    n, k, units, direct, early, shared,
     one_gate, other_gate, one_up, other_up, mix, norm_train, norm_step,
     final_gate, column_gate, column_up, serve_norm, own_up, extra,
     taken, result, mix_held, norm_held, share, raw, mine, heard, partial, whole, gains, gain_rows,
@@ -258,7 +259,7 @@
 
     ones, others = (one_gate, one_up), (other_gate, other_up)
     columns = (column_gate, column_up)
-    odd = leads(col)
+    lead = leads(col)
 
     def peer(d):
         return ((me + d) % n, col)
@@ -324,12 +325,12 @@
 
     e_weight, e_first, e_width = units[early]
     half = cols // 2
-    shared = extra.shape[1]
+    total = extra.shape[1]
     ring = Ring(
         n, rows,
         (
             (final_gate, 0, half, half, None), (final_gate, half, half, half - e_width, None),
-            (extra, 0, shared, shared, odd),
+            (extra, 0, shared, shared, None), (extra, shared, total - shared, total - shared, lead),
         ),
         ring_send, ring_recv,
     )
@@ -404,11 +405,14 @@
     inverse_up = 1.0 / columns[1][...]
     scaled(own_up, 0, 0, cols, inverse_up, held(1, 0, cols))
 
-    @pl.when(odd)
-    def _():
-        scaled(extra, me, 0, shared, inverse_up[:, 0:shared], held(1, 0, shared))
+    def begin_up(b):
+        _, first, width = ring.blocks[b][0:3]
+        scaled(extra, me, first, width, inverse_up[:, first:first + width], held(1, first, width))
         for way in range(2):
-            ring.send(way, 0, 2, 0, shared, own_up.at[:, pl.ds(0, shared)])
+            ring.send(way, 0, b, 0, width, own_up.at[:, pl.ds(first, width)])
+
+    begin_up(2)
+    pl.when(lead)(lambda: begin_up(3))
 
     inverse = 1.0 / columns[e_weight][:, e_first:e_first + e_width]
     wait_for(raw, raw_sem.at[1])
@@ -446,15 +450,15 @@
     return col % 2 == LEADER
 
 
-def second_kernel(n, shared, own_up, after, final_up, ring_send, ring_recv):
+def second_kernel(n, shared, total, own_up, after, final_up, ring_send, ring_recv):
     rows, cols = own_up.shape
-    half = (cols - shared) // 2
+    half = (cols - total) // 2
     even = jnp.logical_not(leads(lax.axis_index("model")))
     ring = Ring(
         n, rows,
         (
-            (final_up, shared, half, half, None), (final_up, shared + half, half, half, None),
-            (final_up, 0, shared, shared, even),
+            (final_up, total, half, half, None), (final_up, total + half, half, half, None),
+            (final_up, shared, total - shared, total - shared, even),
         ),
         ring_send, ring_recv,
     )
@@ -486,21 +490,29 @@
         pltpu.make_async_copy(source.at[span], target.at[span], sem).start()
 
 
-def first_writer(final_gate, column_gate, column_up, serve_norm, extra, gate_out, gate_column, up_column, norm_out, up_out, after, sem):
+def by_role(act, shared, total):
+    lead = leads(lax.axis_index("model"))
+    pl.when(lead)(functools.partial(act, total))
+    pl.when(jnp.logical_not(lead))(functools.partial(act, shared))
+
+
+def first_writer(shared, final_gate, column_gate, column_up, serve_norm, extra, gate_out, gate_column, up_column, norm_out, up_out, after, sem):
     whole = ((final_gate, gate_out), (column_gate, gate_column), (column_up, up_column), (serve_norm, norm_out))
-    lead = leads(lax.axis_index("model"))
-    part = up_out.at[:, pl.ds(0, extra.shape[1])]
     for i, (source, target) in enumerate(whole):
         out(source, target, sem.at[i])
-    pl.when(lead)(lambda: out(extra, part, sem.at[len(whole)]))
     after[...] = jnp.zeros_like(after)
+
+    def write(width):
+        source, target = extra.at[:, pl.ds(0, width)], up_out.at[:, pl.ds(0, width)]
+        out(source, target, sem.at[len(whole)])
+        pltpu.make_async_copy(source, target, sem.at[len(whole)]).wait()
+
+    by_role(write, shared, extra.shape[1])
     for i, (source, target) in enumerate(whole):
         pltpu.make_async_copy(source, target, sem.at[i]).wait()
-    pl.when(lead)(lambda: pltpu.make_async_copy(extra, part, sem.at[len(whole)]).wait())
-
-
-def last_writer(shared, final_up, up_in, up_out, sem):
-    lead = leads(lax.axis_index("model"))
+
+
+def last_writer(shared, total, final_up, up_in, up_out, sem):
     cols = final_up.shape[1]
 
     def write(first):
@@ -508,8 +520,7 @@
         out(final_up.at[:, span], up_out.at[:, span], sem.at[0])
         pltpu.make_async_copy(final_up.at[:, span], up_out.at[:, span], sem.at[0]).wait()
 
-    pl.when(lead)(functools.partial(write, shared))
-    pl.when(jnp.logical_not(lead))(functools.partial(write, 0))
+    by_role(write, shared, total)
 
 
 def solution(mesh):
@@ -539,16 +550,16 @@
         if near:
             block = 2 * cols // n
             e = cols // 16
-            shared = cols // 8 * SHARED
+            shared, total = cols // 8 * SHARED, cols // 8 * (SHARED + MORE)
             units = (
                 (0, 0, block), (0, block, block), (0, 8 * e, 7 * e),
                 (1, 0, 8 * e), (1, 8 * e, 8 * e), (0, 15 * e, e),
             )
             direct, early = 2, len(units) - 1
             final_gate, column_gate, column_up, serve_norm, own_up, extra = pl.pallas_call(
-                functools.partial(near_kernel, n, k, units, direct, early),
+                functools.partial(near_kernel, n, k, units, direct, early, shared),
                 out_shape=[pltpu.VMEM(*shape) for shape in shapes[0:1] + shapes[2:5]] + [
-                    pltpu.VMEM((rows, cols), jnp.bfloat16), pltpu.VMEM((n * rows, shared), jnp.bfloat16),
+                    pltpu.VMEM((rows, cols), jnp.bfloat16), pltpu.VMEM((n * rows, total), jnp.bfloat16),
                 ],
                 in_specs=[hbm] * 7,
                 out_specs=[vmem] * 6,
@@ -564,13 +575,15 @@
                     pltpu.VMEM((n, 1, block + LANES), jnp.float32),
                 ] + gain_shapes + [
                     sems((len(units),)), sems((2,)), sems((2,)), sems((1,)), sems((direct,)), sems((2,)), sems((2,)), sems((2,)),
-                    sems((2, 3)), sems((n // 2, 2, 3)),
+                    sems((2, 4)), sems((n // 2, 2, 4)),
                 ],
-                compiler_params=pltpu.CompilerParams(collective_id=0, has_side_effects=True, vmem_limit_bytes=(54 - SHARED) * 2**20),
+                compiler_params=pltpu.CompilerParams(
+                    collective_id=0, has_side_effects=True, vmem_limit_bytes=(54 - SHARED - MORE) * 2**20
+                ),
             )(*operands)
             full = [jax.ShapeDtypeStruct(*shape) for shape in shapes]
             final_gate, column_gate, column_up, serve_norm, final_up, after = pl.pallas_call(
-                first_writer,
+                functools.partial(first_writer, shared),
                 out_shape=[full[0], full[2], full[3], full[4], full[1], pltpu.VMEM((8, LANES), jnp.float32)],
                 in_specs=[vmem] * 5,
                 out_specs=[hbm] * 5 + [vmem],
@@ -578,7 +591,7 @@
                 compiler_params=pltpu.CompilerParams(vmem_limit_bytes=2**20),
             )(final_gate, column_gate, column_up, serve_norm, extra)
             gathered = pl.pallas_call(
-                functools.partial(second_kernel, n, shared),
+                functools.partial(second_kernel, n, shared, total),
                 out_shape=pltpu.VMEM(*shapes[1]),
                 in_specs=[vmem] * 2,
                 out_specs=vmem,
@@ -586,7 +599,7 @@
                 compiler_params=pltpu.CompilerParams(collective_id=1, has_side_effects=True, vmem_limit_bytes=2**20),
             )(own_up, after)
             final_up = pl.pallas_call(
-                functools.partial(last_writer, shared),
+                functools.partial(last_writer, shared, total),
                 out_shape=full[1],
                 in_specs=[vmem, hbm],
                 out_specs=hbm,

time: 170 us -> 170 us (level)
  no operation moved by 1% of the time
where the time goes in v6:
time: 170 us; the launch traced here: 169 us
  Pallas kernels  169 us (99%)
    pallas_call x1, Pallas kernels, local(): pl.pallas_call(functools.partial(near_kernel, n, k, units, direct, early,...  131 us
    pallas_call x1, Pallas kernels, local(): pl.pallas_call(functools.partial(second_kernel, n, shared, total), out_sh...  31.5 us
    pallas_call x1, Pallas kernels, local(): pl.pallas_call(functools.partial(first_writer, shared), out_shape=[full[0...  4.92 us

profile of v6, /device:TPU:0, one launch (start us, length us, event | category | flops | bytes accessed | tf_op | source)
XLA Modules:
  0.0 169.5 jit_solution(7424527898876341532)
XLA Ops:
  0.6 130.7 %shard_map.110 = (bf16[2048,2048]{1,0:T(8,128)(2,1)S(1)}, f32[1,2048]{1,0:T(1,128)S(1)}, f32[1,2048]{1,0:T(1,128)S(1)}, bf16[16,128]{1,0:T(8,128)(2,1)S(1)}, bf1...) custom-call(f32[256,2048]{1,0:T(8,128)} %one_gate.1, f32[256,2048]{1,0:T(8,128)} %other_gate.1, ...), custom_call_target="tpu_custom_call" | custom-call | tf_op jit(solution)/shard_map/pallas_call | solution.py:559
  131.4 4.9 %shard_map.111 = (bf16[2048,2048]{1,0:T(8,128)(2,1)}, f32[1,2048]{1,0:T(1,128)}, f32[1,2048]{1,0:T(1,128)}, bf16[16,128]{1,0:T(8,128)(2,1)}, bf16[2048,2048]{1,0:T(8,128)(2,1)}, /*index=5*/f32[8,128]{1,0:T(8,128)S(1)}) custom-call(bf16[2048,2048]{1,0:T(8,128)(2,1)S(1)} %get-tuple-element.17.final_gate, f32[1,2048]{1,0:T(1,128)S(1)} %get-tuple-element.18.column_gate, ...), custom_call_target="tpu_custom_call" | custom-call | tf_op jit(solution)/shard_map/pallas_call | solution.py:585
  136.3 31.5 %shard_map.112.final_up = bf16[2048,2048]{1,0:T(8,128)(2,1)S(1)} custom-call(bf16[256,2048]{1,0:T(8,128)(2,1)S(1)} %get-tuple-element.23.own_up, f32[8,128]{1,0:T(8,128)S(1)} %get-tuple-element.24.after), custom_call_target="tpu_custom_call" | custom-call | tf_op jit(solution)/shard_map/pallas_call | solution.py:593
  167.8 1.7 shard_map.113
